TPU v7x, 32 devices: a whole 2x2x4 slice. The times are simulated.
32 devices in a mesh: seq: 8 (over z, y), head: 4 (over x, core).
Axes of the slice: x: 2, y: 2, z: 4, core: 2. Of those that a mesh axis runs over, the one named last changes fastest.
Arguments:
- queries: bfloat16 [2048, 4096], P('seq', 'head'), may hold values from -80 to 80, as said below
- keys_in: bfloat16 [2048, 4096], P('seq', 'head'), may hold values from -4 to 4
- values_in: bfloat16 [2048, 4096], P('seq', 'head'), may hold values from -6 to 6
- out_weight: bfloat16 [4096, 4096], P('head'), may hold values from -0.09375 to 0.09375
- spans: int32 [32], P('head'), may hold values from 1024 to 4096
- full_ids: int32 [8], P('head'), may hold values from 0 to 31, as said below
Outputs:
- mixed: bfloat16 [2048, 4096], P('seq', 'head')
Inputs may be any that keep to these rules, and one draw needn't show every extreme that they name: `queries`: unlike a plain normal draw, some rows may be far larger than the rest. `full_ids`: increasing and distinct; entries g * 2 to (g + 1) * 2 - 1 name heads of group g, that is heads g * 8 to (g + 1) * 8 - 1.
All inputs are finite; a program needn't handle non-finite values.
Results may differ from a plain program's by a relative error of at most 0.012.
Values may be sent and summed in bfloat16 or wider, within the bound.
No kernel may reach another device: no remote copies, remote signals or barrier semaphores. Data moves between devices by JAX's collectives and lax.ppermute only.
A program may use at most 128 MiB of HBM per device.

v0:
```python
import math

import functools

import jax
import jax.numpy as jnp
from jax import lax
from jax.experimental import pallas as pl
from jax.experimental.pallas import tpu as pltpu
from jax.sharding import PartitionSpec as P

HEAD_DIM = 128
SPAN_MAX = 4096


NEG_FILL = -1e30


def from_behind(block, axis, distance):
    devices = range(lax.axis_size(axis))
    route = [(i - distance, i) for i in devices if i - distance in devices]
    return lax.ppermute(block, axis, route)


def online_update(carry_state, scores, allowed, value_rows):
    old_peak, row_total, numerator = carry_state
    masked = jnp.where(allowed, scores, NEG_FILL)
    new_peak = jnp.maximum(old_peak, jnp.max(masked, axis=-1))
    weights = jnp.where(allowed, jnp.exp(masked - new_peak[..., None]), 0.0)
    rescale = jnp.exp(old_peak - new_peak)
    row_total = row_total * rescale + jnp.sum(weights, axis=-1)
    numerator = numerator * rescale[..., None] + jnp.einsum(
        "hqk,hkd->hqd", weights.astype(jnp.bfloat16), value_rows, preferred_element_type=jnp.float32
    )
    return (new_peak, row_total, numerator)


def empty_state(lead_count, row_count, head_width):
    return (
        jnp.full((lead_count, row_count), NEG_FILL, jnp.float32),
        jnp.zeros((lead_count, row_count), jnp.float32),
        jnp.zeros((lead_count, row_count, head_width), jnp.float32),
    )


def finish(carry_state):
    return (carry_state[2] / carry_state[1][..., None]).astype(jnp.bfloat16)


def ring_path(queries, keys_in, values_in, out_weight, spans, full_ids):
    score_scale = HEAD_DIM ** (-0.5)
    n_seq = lax.axis_size("seq")
    seq_index = lax.axis_index("seq")
    tok_rows = queries.shape[0]
    group_heads = queries.shape[1] // HEAD_DIM
    full_count = full_ids.shape[0]
    band_count = group_heads - full_count
    head_base = lax.axis_index("head") * group_heads
    local_range = jnp.arange(group_heads)
    marks = jnp.sum(
        (local_range[:, None] + head_base == full_ids[None, :]).astype(jnp.int32), axis=1
    )
    order_local = jnp.argsort(marks * group_heads + local_range)
    band_local = order_local[:band_count]
    full_local = order_local[band_count:]
    query_three = queries.reshape(tok_rows, group_heads, HEAD_DIM)
    key_three = keys_in.reshape(tok_rows, group_heads, HEAD_DIM)
    value_three = values_in.reshape(tok_rows, group_heads, HEAD_DIM)
    query_band = jnp.take(query_three, band_local, axis=1).transpose(1, 0, 2)
    kv_band = jnp.stack(
        [
            jnp.take(key_three, band_local, axis=1).transpose(1, 0, 2),
            jnp.take(value_three, band_local, axis=1).transpose(1, 0, 2),
        ]
    )
    band_reach = jnp.take(spans, band_local)
    query_pos = seq_index * tok_rows + jnp.arange(tok_rows)
    hop_count = min(max(1, SPAN_MAX // tok_rows), n_seq - 1)
    arrived = [(kv_band, 0)]
    moving = kv_band
    for distance in range(1, hop_count + 1):
        moving = from_behind(moving, "seq", 1)
        arrived.append((moving, distance))
    batch_size = max(1, 512 // tok_rows)
    band_state = empty_state(band_count, tok_rows, HEAD_DIM)
    for first_piece in range(0, len(arrived), batch_size):
        batch_pieces = arrived[first_piece : first_piece + batch_size]
        key_rows = jnp.concatenate([arrival[0][0] for arrival in batch_pieces], axis=1)
        value_rows = jnp.concatenate([arrival[0][1] for arrival in batch_pieces], axis=1)
        key_pos = jnp.concatenate(
            [(seq_index - arrival[1]) * tok_rows + jnp.arange(tok_rows) for arrival in batch_pieces]
        )
        scores = (
            jnp.einsum("hqd,hkd->hqk", query_band, key_rows, preferred_element_type=jnp.float32)
            * score_scale
        )
        gap_size = query_pos[None, :, None] - key_pos[None, None, :]
        allowed = (
            (gap_size >= 0) & (gap_size < band_reach[:, None, None]) & (key_pos >= 0)[None, None, :]
        )
        band_state = online_update(band_state, scores, allowed, value_rows)
    band_out = finish(band_state)
    query_full = jnp.take(query_three, full_local, axis=1).transpose(1, 0, 2)
    key_full = jnp.take(key_three, full_local, axis=1).transpose(1, 0, 2)
    value_full = jnp.take(value_three, full_local, axis=1).transpose(1, 0, 2)
    kv_full = jnp.stack([key_full, value_full])
    last_query = seq_index * tok_rows + tok_rows - 1
    key_piece = lax.all_gather(kv_full, "seq", axis=2, tiled=True)
    row_count = key_piece.shape[2]
    tile_rows = math.gcd(row_count, 512)

    def absorb_tile(tile_index, inner_state):
        key_tile = lax.dynamic_slice_in_dim(key_piece[0], tile_index * tile_rows, tile_rows, 1)
        value_tile = lax.dynamic_slice_in_dim(key_piece[1], tile_index * tile_rows, tile_rows, 1)
        key_pos = tile_index * tile_rows + jnp.arange(tile_rows)
        scores = (
            jnp.einsum("hqd,hkd->hqk", query_full, key_tile, preferred_element_type=jnp.float32)
            * score_scale
        )
        allowed = key_pos[None, None, :] <= query_pos[None, :, None]
        return online_update(inner_state, scores, allowed, value_tile)

    live_tiles = jnp.clip(last_query // tile_rows + 1, 0, row_count // tile_rows)
    full_state = lax.fori_loop(
        0, live_tiles, absorb_tile, empty_state(full_count, tok_rows, HEAD_DIM)
    )
    full_out = finish(full_state)
    combined = jnp.concatenate([band_out, full_out], axis=0)
    inverse = jnp.argsort(order_local)
    per_head = jnp.take(combined, inverse, axis=0)
    attended = per_head.transpose(1, 0, 2).reshape(tok_rows, group_heads * HEAD_DIM)
    projected = jnp.dot(attended, out_weight, preferred_element_type=jnp.float32)
    return lax.psum_scatter(projected.astype(jnp.bfloat16), "head", scatter_dimension=1, tiled=True)


def move(block, axis, pairs):
    return lax.ppermute(block, axis, pairs)


def swap(block, axis, flip):
    return move(block, axis, [(i, i ^ flip) for i in range(lax.axis_size(axis))])


def in_vmem(count):
    return [pl.BlockSpec(memory_space=pltpu.VMEM)] * count


def held(array):
    return pltpu.with_memory_space_constraint(array, pltpu.VMEM)


SMEM = pl.BlockSpec(memory_space=pltpu.SMEM)
FACTOR = HEAD_DIM**-0.5 * math.log2(math.e)
STAT_ROWS = 16


def own_kernel(body, out_shapes, in_specs, scratch=(), flops=10**8, limit=20 * 2**20):
    return pl.pallas_call(
        body,
        out_shape=out_shapes,
        in_specs=in_specs,
        out_specs=in_vmem(len(out_shapes)),
        scratch_shapes=list(scratch),
        compiler_params=pltpu.CompilerParams(vmem_limit_bytes=limit),
        cost_estimate=pl.CostEstimate(flops=flops, bytes_accessed=10**6, transcendentals=0),
    )


def deal(half, me_ref, spans_ref, full_ref, q_ref, k_ref, v_ref, *refs):
    reach_ref, sems, spans, full_ids = refs[4 * half :]
    me = me_ref[0]
    low = me % half
    tables = [
        pltpu.make_async_copy(spans_ref, spans, sems.at[8 * half]),
        pltpu.make_async_copy(full_ref, full_ids, sems.at[8 * half + 1]),
    ]
    for copy in tables:
        copy.start()
    rows = q_ref.shape[0]
    waits = []

    def fetch(source, head, out_ref, place):
        at = pl.multiple_of(head * HEAD_DIM, HEAD_DIM)
        return pltpu.make_async_copy(
            source.at[:, pl.ds(at, HEAD_DIM)],
            out_ref.at[pl.ds(place * rows, rows)],
            sems.at[len(waits)],
        )

    for upper in range(2):
        inner = refs[2 * upper * half : (2 * upper + 1) * half]
        cross = refs[(2 * upper + 1) * half : (2 * upper + 2) * half]
        for flip in range(half - 1, -1, -1):
            for place, source in enumerate((q_ref, k_ref, v_ref)):
                copy = fetch(source, (low ^ flip) + upper * half, inner[flip], place)
                copy.start()
                waits.append(copy)
        for flip in range(half - 1, -1, -1):
            target = low ^ flip
            if upper:
                copy = fetch(v_ref, target + half, cross[flip], 0)
                copy.start()
            else:
                below = fetch(k_ref, target + half, cross[flip], 0)
                copy = fetch(q_ref, target, cross[flip], 0)
                pl.when(me < half)(below.start)
                pl.when(me >= half)(copy.start)
            waits.append(copy)
    for copy in tables:
        copy.wait()
    for upper in range(2):
        local = low + upper * half
        reach = spans[local]
        for place in range(full_ids.shape[0]):
            is_full = full_ids[place] == me_ref[1] * 2 * half + local
            reach = jnp.where(is_full, 2 * half * rows, reach)
        reach_ref[upper : upper + 1] = jnp.full((1, reach_ref.shape[1]), reach, jnp.int32)
    for copy in waits:
        copy.wait()


def square_eye(size):
    row = lax.broadcasted_iota(jnp.int32, (size, size), 0)
    return row == lax.broadcasted_iota(jnp.int32, (size, size), 1)


def pack_stat(stat):
    eye = square_eye(HEAD_DIM)
    rows = []
    for first in range(0, stat.shape[0], HEAD_DIM):
        piece = jnp.where(eye, stat[first : first + HEAD_DIM], 0.0)
        left = jnp.sum(piece, axis=0, keepdims=True)
        for _ in range(3):
            part = left.astype(jnp.bfloat16).astype(jnp.float32)
            rows.append(part)
            left = left - part
    rows.append(jnp.zeros((STAT_ROWS - len(rows), HEAD_DIM), jnp.float32))
    return jnp.concatenate(rows, axis=0).astype(jnp.bfloat16)


def share_column(here, there, size):
    eye = square_eye(HEAD_DIM)
    apart = there.astype(jnp.float32) - here.astype(jnp.float32)
    columns = []
    for index in range(size // HEAD_DIM):
        row = apart[3 * index : 3 * index + 1]
        for more in (1, 2):
            row = row + apart[3 * index + more : 3 * index + more + 1]
        share = 1.0 / (1.0 + jnp.exp2(row))
        columns.append(jnp.sum(jnp.where(eye, share, 0.0), axis=1, keepdims=True))
    return jnp.concatenate(columns, axis=0)


def softmax_rows(pieces, value_tiles):
    peak = jnp.max(functools.reduce(jnp.maximum, pieces), axis=1, keepdims=True)
    total, numerator = None, None
    for scores, value_tile in zip(pieces, value_tiles):
        weights = jnp.exp2((scores - peak) * FACTOR)
        total = weights if total is None else total + weights
        product = jnp.dot(
            weights.astype(jnp.bfloat16), value_tile, preferred_element_type=jnp.float32
        )
        numerator = product if numerator is None else numerator + product
    return numerator, jnp.sum(total, axis=1, keepdims=True), peak


def score_tile(q_tile, k_tile):
    return lax.dot_general(
        q_tile, k_tile, (((1,), (1,)), ((), ())), preferred_element_type=jnp.float32
    )


def gaps(block):
    row = lax.broadcasted_iota(jnp.int32, (block, block), 0)
    return row - lax.broadcasted_iota(jnp.int32, (block, block), 1)


def gather_rows(half, low, inner, qkv, first):
    block = inner[0].shape[0] // 3
    for flip in range(half):
        at = pl.multiple_of((low ^ flip) * block, block)
        for place in range(3):
            rows = slice(place * block, (place + 1) * block)
            qkv[first + place, pl.ds(at, block)] = inner[flip][rows]


def own_pieces(qkv, first, i, gap):
    block = gap.shape[0]
    q_tile = qkv[first, i * block : (i + 1) * block]
    pieces, value_tiles = [], []
    for j in range(i + 1):
        scores = score_tile(q_tile, qkv[first + 1, j * block : (j + 1) * block])
        pieces.append(jnp.where(gap >= 0, scores, NEG_FILL) if i == j else scores)
        value_tiles.append(qkv[first + 2, j * block : (j + 1) * block])
    return q_tile, pieces, value_tiles


def attend_lower_own(half, qkv, gap, o_low, stats):
    for i in range(half):
        numerator, total, peak = softmax_rows(*own_pieces(qkv, 0, i, gap)[1:])
        o_low[i] = (numerator / total).astype(jnp.bfloat16)
        stats[i] = pack_stat(peak * FACTOR + jnp.log2(total))


def attend_low(half, me_ref, reach_ref, *refs):
    inner, cross, out_refs = refs[:half], refs[half : 2 * half], refs[2 * half : 3 * half]
    o_low, stats, qkv = refs[3 * half :]
    block = cross[0].shape[0]
    low = me_ref[0] % half
    gap = gaps(block)

    @pl.when(me_ref[0] < half)
    def _():
        reach = reach_ref[0:1]
        for flip in range(half - 1, -1, -1):
            pieces = []
            for other in range(half):
                offset = (half + (low ^ flip) - (low ^ other)) * block
                scores = score_tile(cross[flip][...], inner[other][block : 2 * block])
                pieces.append(jnp.where(gap < reach - offset, scores, NEG_FILL))
            value_tiles = [inner[other][2 * block :] for other in range(half)]
            numerator, total, peak = softmax_rows(pieces, value_tiles)
            out_refs[flip][:block] = (numerator / total).astype(jnp.bfloat16)
            out_refs[flip][block:] = pack_stat(peak * FACTOR + jnp.log2(total))

    @pl.when(me_ref[0] >= half)
    def _():
        gather_rows(half, low, inner, qkv, 0)
        attend_lower_own(half, qkv, gap, o_low, stats)


def attend_rest(half, me_ref, reach_ref, low_ref, stat_ref, *refs):
    lower, upper = refs[:half], refs[half : 2 * half]
    cross_k, cross_v = refs[2 * half : 3 * half], refs[3 * half : 4 * half]
    out_refs = refs[4 * half : 5 * half]
    qkv, o_low, o_up, stats = refs[5 * half :]
    me = me_ref[0]
    low = me % half
    block = cross_k[0].shape[0]
    gap = gaps(block)
    gather_rows(half, low, upper, qkv, 3)

    @pl.when(me < half)
    def _():
        gather_rows(half, low, lower, qkv, 0)
        attend_lower_own(half, qkv, gap, o_low, stats)
        for i in range(half):
            numerator, total, _ = softmax_rows(*own_pieces(qkv, 3, i, gap)[1:])
            o_up[i] = (numerator / total).astype(jnp.bfloat16)
        for flip in range(half):
            out_refs[flip][:block] = o_low[low ^ flip]
            out_refs[flip][2 * block :] = stats[low ^ flip]

    @pl.when(me >= half)
    def _():
        reach = reach_ref[1:2]
        for i in range(half):
            q_tile, pieces, value_tiles = own_pieces(qkv, 3, i, gap)
            for other in range(half):
                offset = (half + i - (low ^ other)) * block
                scores = score_tile(q_tile, cross_k[other][...])
                pieces.append(jnp.where(gap < reach - offset, scores, NEG_FILL))
                value_tiles.append(cross_v[other][...])
            numerator, total, _ = softmax_rows(pieces, value_tiles)
            o_up[i] = (numerator / total).astype(jnp.bfloat16)
        for flip in range(half):
            out_refs[flip][:block] = low_ref[low ^ flip]
            out_refs[flip][2 * block :] = stat_ref[low ^ flip]

    for flip in range(half):
        out_refs[flip][block : 2 * block] = o_up[low ^ flip]


def join_heads(half, me_ref, inner, across, joined):
    me = me_ref[0]
    low = me % half
    block = joined.shape[0]
    for flip in range(half):
        at = pl.multiple_of((low ^ flip) * HEAD_DIM, HEAD_DIM)
        up_at = pl.multiple_of((low ^ flip) * HEAD_DIM + half * HEAD_DIM, HEAD_DIM)
        joined[:, pl.ds(up_at, HEAD_DIM)] = inner[flip][block : 2 * block]

        @pl.when(me < half)
        def _():
            joined[:, pl.ds(at, HEAD_DIM)] = inner[flip][:block]

        @pl.when(me >= half)
        def _():
            share = share_column(inner[flip][2 * block :], across[flip][block:], block)
            mixed = inner[flip][:block].astype(jnp.float32) * share
            mixed = mixed + across[flip][:block].astype(jnp.float32) * (1.0 - share)
            joined[:, pl.ds(at, HEAD_DIM)] = mixed.astype(jnp.bfloat16)


def join_and_project(half, flip, part, parts, me_ref, *refs):
    inner, across, (w_ref, out_ref, joined) = refs[:half], refs[half : 2 * half], refs[2 * half :]
    join_heads(half, me_ref, inner, across, joined)
    project(flip, part, parts, me_ref, joined, w_ref, out_ref)


def project(flip, part, parts, me_ref, joined, w_ref, *refs):
    *other, out_ref = refs
    width = out_ref.shape[1]
    at = pl.multiple_of(((me_ref[1] ^ flip) * parts + part) * width, width)
    product = jnp.dot(
        joined[...], w_ref[:, pl.ds(at, width)], preferred_element_type=jnp.float32
    ).astype(jnp.bfloat16)
    if other:
        total = product.astype(jnp.float32) + other[0][...].astype(jnp.float32)
        product = total.astype(jnp.bfloat16)
    out_ref[...] = product


def half_path(queries, keys_in, values_in, out_weight, spans, full_ids):
    n_seq = lax.axis_size("seq")
    half = n_seq // 2
    bf16, f32 = jnp.bfloat16, jnp.float32
    shape = jax.ShapeDtypeStruct
    where = jnp.stack([lax.axis_index("seq"), lax.axis_index("head")]).astype(jnp.int32)
    block = queries.shape[0]
    down = range(half - 1, -1, -1)
    piece = shape((block, HEAD_DIM), bf16)

    hbm = pl.BlockSpec(memory_space=pltpu.HBM)
    ours = (spans, full_ids, queries, keys_in, values_in)
    ours = [pltpu.with_memory_space_constraint(a, pltpu.HBM) for a in ours]
    dealt = own_kernel(
        functools.partial(deal, half),
        ([shape((3 * block, HEAD_DIM), bf16)] * half + [piece] * half) * 2
        + [shape((8, block), jnp.int32)],
        [SMEM] + [hbm] * 5,
        [
            pltpu.SemaphoreType.DMA((8 * half + 2,)),
            pltpu.SMEM(spans.shape, jnp.int32),
            pltpu.SMEM(full_ids.shape, jnp.int32),
        ],
    )(where, *ours)
    reach = held(dealt[4 * half])
    inner = [list(dealt[:half]), list(dealt[2 * half : 3 * half])]
    cross = [list(dealt[half : 2 * half]), list(dealt[3 * half : 4 * half])]
    for upper in range(2):
        for flip in range(half - 1, 0, -1):
            inner[upper][flip] = swap(inner[upper][flip], "seq", flip)
        for flip in down:
            pairs = [(i, i ^ half ^ flip) for i in range(half if upper else n_seq)]
            cross[upper][flip] = move(cross[upper][flip], "seq", pairs)
    w_held = held(out_weight)
    inner = [[held(a) for a in arrays] for arrays in inner]
    cross = [[held(a) for a in arrays] for arrays in cross]
    across, own_half = [None] * half, [None] * half
    *lows, o_low, stats = own_kernel(
        functools.partial(attend_low, half),
        [shape((block + STAT_ROWS, HEAD_DIM), bf16)] * half
        + [shape((half, block, HEAD_DIM), bf16), shape((half, STAT_ROWS, HEAD_DIM), bf16)],
        [SMEM] + in_vmem(1 + 2 * half),
        [pltpu.VMEM((3, half * block, HEAD_DIM), bf16)],
        flops=2 * 10**9,
    )(where, reach, *inner[0], *cross[0])
    for flip in range(half):
        pairs = [(i, half + (i ^ flip)) for i in range(half)]
        across[flip] = move(lows[flip], "seq", pairs)
    rest = own_kernel(
        functools.partial(attend_rest, half),
        [shape((2 * block + STAT_ROWS, HEAD_DIM), bf16)] * half,
        [SMEM] + in_vmem(3 + 4 * half),
        [
            pltpu.VMEM((6, half * block, HEAD_DIM), bf16),
            pltpu.VMEM((half, block, HEAD_DIM), bf16),
            pltpu.VMEM((half, block, HEAD_DIM), bf16),
            pltpu.VMEM((half, STAT_ROWS, HEAD_DIM), bf16),
        ],
        flops=4 * 10**9,
    )(where, reach, held(o_low), held(stats), *inner[0], *inner[1], *cross[0], *cross[1])
    for flip in range(half):
        own_half[flip] = swap(rest[flip], "seq", flip) if flip else rest[flip]
    came = [held(a) for a in own_half + across]
    width = out_weight.shape[1] // lax.axis_size("head")
    parts = 2
    slab = shape((block, width // parts), bf16)

    def columns_of(flip, part, parts, rows, *other):
        return own_kernel(
            functools.partial(project, flip, part, parts),
            [shape((block, width // parts), bf16)],
            [SMEM] + in_vmem(2 + len(other)),
            flops=10**9 // parts,
        )(where, held(rows), w_held, *[held(a) for a in other])[0]

    first, joined = own_kernel(
        functools.partial(join_and_project, half, 3, 0, parts),
        [slab, shape((block, n_seq * HEAD_DIM), bf16)],
        [SMEM] + in_vmem(2 * half + 1),
        flops=10**9,
    )(where, *came, w_held)
    first = swap(first, "head", 1)
    second = columns_of(3, 1, parts, joined)
    second = swap(second, "head", 1)
    far = [first, second]
    for part in range(parts):
        far[part] = columns_of(2, part, parts, joined, far[part])
    rows, _ = lax.optimization_barrier((joined, far[1]))
    for part in range(parts):
        far[part] = swap(far[part], "head", 2)
    near = columns_of(1, 0, 1, rows)
    near = columns_of(0, 0, 1, rows, swap(near, "head", 1))
    return (near.astype(f32) + jnp.concatenate(far, axis=1).astype(f32)).astype(bf16)


def on_device(queries, keys_in, values_in, out_weight, spans, full_ids):
    n_seq, n_head = lax.axis_size("seq"), lax.axis_size("head")
    block = queries.shape[0]
    one_head_each = queries.shape[1] == n_seq * HEAD_DIM
    if one_head_each and n_head == 4 and n_seq == 8 and block == 256:
        return half_path(queries, keys_in, values_in, out_weight, spans, full_ids)
    return ring_path(queries, keys_in, values_in, out_weight, spans, full_ids)


def solution(mesh):
    placed = (
        P("seq", "head"),
        P("seq", "head"),
        P("seq", "head"),
        P("head", None),
        P("head"),
        P("head"),
    )
    return jax.shard_map(
        on_device, mesh=mesh, in_specs=placed, out_specs=P("seq", "head"), check_vma=False
    )
```

profile of v0, /device:TPU:0, one launch (start us, length us, event | category | flops | bytes accessed | tf_op | source)
XLA Modules:
  0.0 83.3 jit_solution(16820412890585452310)
XLA Ops:
  0.1 2.5 %shard_map.64 = (bf16[768,128]{1,0:T(8,128)(2,1)S(1)}, bf16[768,128]{1,0:T(8,128)(2,1)S(1)}, bf16[768,128]{1,0:T(8,128)(2,1)S(1)}, bf16[768,128]{1,0:T(8,128)(2,...) custom-call(s32[2]{0:T(128)S(1)} %pad_add_fusion.me_ref, ...), custom_call_target="tpu_custom_call" | custom-call | flops 100000000 | bytes 1000000 | tf_op jit(solution)/shard_map/pallas_call | solution.py:427
  2.6 4.1 %collective-permute-start.3 = (bf16[256,128]{1,0:T(8,128)(2,1)S(1)}, bf16[256,128]{1,0:T(8,128)(2,1)S(1)}, u32[]{:S(2)}, u32[]{:S(2)}) collective-permute-start(bf16[256,128]{1,0:T(8,128)(2,1)S(1)} %get-tuple-element.40), channel_id=1, source_target_pairs={{0,16},{4,20},{8,24},{12,28},{16,0},{20,4},{24,8},{28,12},{1,17},{... | collective-permute-start | bytes 196616 | tf_op jit(solution)/shard_map/ppermute | solution.py:137
  8.2 1.8 %collective-permute-start.1 = (bf16[768,128]{1,0:T(8,128)(2,1)S(1)}, bf16[768,128]{1,0:T(8,128)(2,1)S(1)}, u32[]{:S(2)}, u32[]{:S(2)}) collective-permute-start(bf16[768,128]{1,0:T(8,128)(2,1)S(1)} %get-tuple-element.38), channel_id=1, source_target_pairs={{0,8},{4,12},{8,0},{12,4},{16,24},{20,28},{24,16},{28,20},{1,9},{5... | collective-permute-start | bytes 589832 | tf_op jit(solution)/shard_map/ppermute | solution.py:137
  10.1 1.4 %collective-permute-start.2 = (bf16[768,128]{1,0:T(8,128)(2,1)S(1)}, bf16[768,128]{1,0:T(8,128)(2,1)S(1)}, u32[]{:S(2)}, u32[]{:S(2)}) collective-permute-start(bf16[768,128]{1,0:T(8,128)(2,1)S(1)} %get-tuple-element.39), channel_id=1, source_target_pairs={{0,12},{4,8},{8,4},{12,0},{16,28},{20,24},{24,20},{28,16},{1,13},{... | collective-permute-start | bytes 589832 | tf_op jit(solution)/shard_map/ppermute | solution.py:137
  11.5 4.1 %collective-permute-start.5 = (bf16[256,128]{1,0:T(8,128)(2,1)S(1)}, bf16[256,128]{1,0:T(8,128)(2,1)S(1)}, u32[]{:S(2)}, u32[]{:S(2)}) collective-permute-start(bf16[256,128]{1,0:T(8,128)(2,1)S(1)} %get-tuple-element.42), channel_id=1, source_target_pairs={{0,24},{4,28},{8,16},{12,20},{16,8},{20,12},{24,0},{28,4},{1,25},{... | collective-permute-start | bytes 196616 | tf_op jit(solution)/shard_map/ppermute | solution.py:137
  15.6 2.2 %collective-permute-start.6 = (bf16[256,128]{1,0:T(8,128)(2,1)S(1)}, bf16[256,128]{1,0:T(8,128)(2,1)S(1)}, u32[]{:S(2)}, u32[]{:S(2)}) collective-permute-start(bf16[256,128]{1,0:T(8,128)(2,1)S(1)} %get-tuple-element.43), channel_id=1, source_target_pairs={{0,28},{4,24},{8,20},{12,16},{16,12},{20,8},{24,4},{28,0},{1,29},{... | collective-permute-start | bytes 196616 | tf_op jit(solution)/shard_map/ppermute | solution.py:137
  17.8 6.1 %collective-permute-done.5.refs_6_.refs_10_ = bf16[256,128]{1,0:T(8,128)(2,1)S(1)} collective-permute-done((bf16[256,128]{1,0:T(8,128)(2,1)S(1)}, bf16[256,128]{1,0:T(8,128)(2,1)S(1)}, u32[]{:S(2)}, u32[]{:S(2)}) %collective-permute-start.5) | collective-permute-done | bytes 65568 | tf_op jit(solution)/shard_map/ppermute | solution.py:137
  28.4 2.8 %collective-permute-start.8 = (bf16[768,128]{1,0:T(8,128)(2,1)S(1)}, bf16[768,128]{1,0:T(8,128)(2,1)S(1)}, u32[]{:S(2)}, u32[]{:S(2)}) collective-permute-start(bf16[768,128]{1,0:T(8,128)(2,1)S(1)} %get-tuple-element.48), channel_id=1, source_target_pairs={{0,8},{4,12},{8,0},{12,4},{16,24},{20,28},{24,16},{28,20},{1,9},{5... | collective-permute-start | bytes 589832 | tf_op jit(solution)/shard_map/ppermute | solution.py:137
  32.1 6.9 %collective-permute-start.12 = (bf16[256,128]{1,0:T(8,128)(2,1)S(1)}, bf16[256,128]{1,0:T(8,128)(2,1)S(1)}, u32[]{:S(2)}, u32[]{:S(2)}) collective-permute-start(bf16[256,128]{1,0:T(8,128)(2,1)S(1)} %get-tuple-element.52), channel_id=1, source_target_pairs={{0,24},{4,28},{8,16},{12,20},{1,25},{5,29},{9,17},{13,21},{2,26},{... | collective-permute-start | bytes 196616 | tf_op jit(solution)/shard_map/ppermute | solution.py:137
  39.0 1.5 %collective-permute-start.13 = (bf16[256,128]{1,0:T(8,128)(2,1)S(1)}, bf16[256,128]{1,0:T(8,128)(2,1)S(1)}, u32[]{:S(2)}, u32[]{:S(2)}) collective-permute-start(bf16[256,128]{1,0:T(8,128)(2,1)S(1)} %get-tuple-element.53), channel_id=1, source_target_pairs={{0,28},{4,24},{8,20},{12,16},{1,29},{5,25},{9,21},{13,17},{2,30},{... | collective-permute-start | bytes 196616 | tf_op jit(solution)/shard_map/ppermute | solution.py:137
  40.6 2.7 %shard_map.65 = (bf16[272,128]{1,0:T(8,128)(2,1)S(1)}, bf16[272,128]{1,0:T(8,128)(2,1)S(1)}, bf16[272,128]{1,0:T(8,128)(2,1)S(1)}, bf16[272,128]{1,0:T(8,128)(2,...) custom-call(s32[2]{0:T(128)S(1)} %pad_add_fusion.me_ref, ...), custom_call_target="tpu_custom_call" | custom-call | flops 2000000000 | bytes 1000000 | tf_op jit(solution)/shard_map/pallas_call | solution.py:451
  43.3 1.3 %collective-permute-start.17 = (bf16[272,128]{1,0:T(8,128)(2,1)S(1)}, bf16[272,128]{1,0:T(8,128)(2,1)S(1)}, u32[]{:S(2)}, u32[]{:S(2)}) collective-permute-start(bf16[272,128]{1,0:T(8,128)(2,1)S(1)} %get-tuple-element.58), channel_id=1, source_target_pairs={{0,16},{4,20},{8,24},{12,28},{1,17},{5,21},{9,25},{13,29},{2,18},{... | collective-permute-start | bytes 208904 | tf_op jit(solution)/shard_map/ppermute | solution.py:137
  44.6 2.7 %collective-permute-start.18 = (bf16[272,128]{1,0:T(8,128)(2,1)S(1)}, bf16[272,128]{1,0:T(8,128)(2,1)S(1)}, u32[]{:S(2)}, u32[]{:S(2)}) collective-permute-start(bf16[272,128]{1,0:T(8,128)(2,1)S(1)} %get-tuple-element.59), channel_id=1, source_target_pairs={{0,20},{4,16},{8,28},{12,24},{1,21},{5,17},{9,29},{13,25},{2,22},{... | collective-permute-start | bytes 208904 | tf_op jit(solution)/shard_map/ppermute | solution.py:137
  47.3 4.0 %shard_map.66 = (bf16[528,128]{1,0:T(8,128)(2,1)S(1)}, bf16[528,128]{1,0:T(8,128)(2,1)S(1)}, bf16[528,128]{1,0:T(8,128)(2,1)S(1)}, bf16[528,128]{1,0:T(8,128)(2,1)S(1)}) custom-call(s32[2]{0:T(128)S(1)} %pad_add_fusion.me_ref, s32[8,256]{1,0:T(8,128)S(1)} %get-tuple-element.35.reach_ref, bf16[4,256,128]{2,1,0:T(8,128)(2,1)S(1)} %get-tuple-element.44.low_ref, ...), custom_call_target="tpu_custom_call" | custom-call | flops 4000000000 | bytes 1000000 | tf_op jit(solution)/shard_map/pallas_call | solution.py:462
  52.6 2.9 %collective-permute-start.15 = (bf16[528,128]{1,0:T(8,128)(2,1)S(1)}, bf16[528,128]{1,0:T(8,128)(2,1)S(1)}, u32[]{:S(2)}, u32[]{:S(2)}) collective-permute-start(bf16[528,128]{1,0:T(8,128)(2,1)S(1)} %get-tuple-element.56), channel_id=1, source_target_pairs={{0,8},{4,12},{8,0},{12,4},{16,24},{20,28},{24,16},{28,20},{1,9},{5... | collective-permute-start | bytes 405512 | tf_op jit(solution)/shard_map/ppermute | solution.py:137
  55.6 2.4 %collective-permute-start.19 = (bf16[272,128]{1,0:T(8,128)(2,1)S(1)}, bf16[272,128]{1,0:T(8,128)(2,1)S(1)}, u32[]{:S(2)}, u32[]{:S(2)}) collective-permute-start(bf16[272,128]{1,0:T(8,128)(2,1)S(1)} %get-tuple-element.60), channel_id=1, source_target_pairs={{0,24},{4,28},{8,16},{12,20},{1,25},{5,29},{9,17},{13,21},{2,26},{... | collective-permute-start | bytes 208904 | tf_op jit(solution)/shard_map/ppermute | solution.py:137
  58.0 1.4 %collective-permute-start.20 = (bf16[272,128]{1,0:T(8,128)(2,1)S(1)}, bf16[272,128]{1,0:T(8,128)(2,1)S(1)}, u32[]{:S(2)}, u32[]{:S(2)}) collective-permute-start(bf16[272,128]{1,0:T(8,128)(2,1)S(1)} %get-tuple-element.61), channel_id=1, source_target_pairs={{0,28},{4,24},{8,20},{12,16},{1,29},{5,25},{9,21},{13,17},{2,30},{... | collective-permute-start | bytes 208904 | tf_op jit(solution)/shard_map/ppermute | solution.py:137
  59.5 1.3 %collective-permute-done.19.refs_6_ = bf16[272,128]{1,0:T(8,128)(2,1)S(1)} collective-permute-done((bf16[272,128]{1,0:T(8,128)(2,1)S(1)}, bf16[272,128]{1,0:T(8,128)(2,1)S(1)}, u32[]{:S(2)}, u32[]{:S(2)}) %collective-permute-start.19) | collective-permute-done | bytes 69664 | tf_op jit(solution)/shard_map/ppermute | solution.py:137
  61.6 1.3 %shard_map.67 = (bf16[256,512]{1,0:T(8,128)(2,1)S(1)}, bf16[256,1024]{1,0:T(8,128)(2,1)S(1)}) custom-call(s32[2]{0:T(128)S(1)} %pad_add_fusion.me_ref, bf16[528,128]{1,0:T(8,128)(2,1)S(1)} %get-tuple-element.54.refs_0_, bf16[528,128]{1,0:T(8,128)(2,1)S(1)} %collective-permute-done.14.refs_1_, bf16[528,128]{1,0:T(8,128)(2,1)S(1)} %collective-permute-done.15.refs_2_, ...), custom_call_target="tpu_custom_call" | custom-call | flops 1000000000 | bytes 1000000 | tf_op jit(solution)/shard_map/pallas_call | solution.py:489
  64.0 1.5 %collective-permute-done.21.refs_0_ = bf16[256,512]{1,0:T(8,128)(2,1)S(1)} collective-permute-done((bf16[256,512]{1,0:T(8,128)(2,1)S(1)}, bf16[256,512]{1,0:T(8,128)(2,1)S(1)}, u32[]{:S(2)}, u32[]{:S(2)}) %collective-permute-start.21) | collective-permute-done | bytes 262176 | tf_op jit(solution)/shard_map/ppermute | solution.py:137
  68.4 1.5 %collective-permute-start.25 = (bf16[256,512]{1,0:T(8,128)(2,1)S(1)}, bf16[256,512]{1,0:T(8,128)(2,1)S(1)}, u32[]{:S(2)}, u32[]{:S(2)}) collective-permute-start(bf16[256,512]{1,0:T(8,128)(2,1)S(1)} %shard_map.69), channel_id=1, source_target_pairs={{0,2},{1,3},{2,0},{3,1},{4,6},{5,7},{6,4},{7,5},{8,10},{9,11},{10,... | collective-permute-start | bytes 786440 | tf_op jit(solution)/shard_map/ppermute | solution.py:137
  71.1 1.6 %collective-permute-start.24 = (bf16[256,512]{1,0:T(8,128)(2,1)S(1)}, bf16[256,512]{1,0:T(8,128)(2,1)S(1)}, u32[]{:S(2)}, u32[]{:S(2)}) collective-permute-start(bf16[256,512]{1,0:T(8,128)(2,1)S(1)} %shard_map.72), channel_id=1, source_target_pairs={{0,2},{1,3},{2,0},{3,1},{4,6},{5,7},{6,4},{7,5},{8,10},{9,11},{10,... | collective-permute-start | bytes 786440 | tf_op jit(solution)/shard_map/ppermute | solution.py:137
  74.0 3.6 %collective-permute-done.25 = bf16[256,512]{1,0:T(8,128)(2,1)S(1)} collective-permute-done((bf16[256,512]{1,0:T(8,128)(2,1)S(1)}, bf16[256,512]{1,0:T(8,128)(2,1)S(1)}, u32[]{:S(2)}, u32[]{:S(2)}) %collective-permute-start.25) | collective-permute-done | bytes 262176 | tf_op jit(solution)/shard_map/ppermute | solution.py:137
  77.5 4.8 %collective-permute-done.24 = bf16[256,512]{1,0:T(8,128)(2,1)S(1)} collective-permute-done((bf16[256,512]{1,0:T(8,128)(2,1)S(1)}, bf16[256,512]{1,0:T(8,128)(2,1)S(1)}, u32[]{:S(2)}, u32[]{:S(2)}) %collective-permute-start.24) | collective-permute-done | bytes 262176 | tf_op jit(solution)/shard_map/ppermute | solution.py:137
  (44 shorter events, 16.4 us)
Async XLA Ops:
  2.6 8.9 %collective-permute-start.3 = (bf16[256,128]{1,0:T(8,128)(2,1)S(1)}, bf16[256,128]{1,0:T(8,128)(2,1)S(1)}, u32[]{:S(2)}, u32[]{:S(2)}) collective-permute-start(bf16[256,128]{1,0:T(8,128)(2,1)S(1)} %get-tuple-element.40), channel_id=1, source_target_pairs={{0,16},{4,20},{8,24},{12,28},{16,0},{20,4},{24,8},{28,12},{1,17},{... | collective-permute-start | bytes 196616 | tf_op jit(solution)/shard_map/ppermute | solution.py:137
  6.7 8.9 %collective-permute-start.4 = (bf16[256,128]{1,0:T(8,128)(2,1)S(1)}, bf16[256,128]{1,0:T(8,128)(2,1)S(1)}, u32[]{:S(2)}, u32[]{:S(2)}) collective-permute-start(bf16[256,128]{1,0:T(8,128)(2,1)S(1)} %get-tuple-element.41), channel_id=1, source_target_pairs={{0,20},{4,16},{8,28},{12,24},{16,4},{20,0},{24,12},{28,8},{1,21},{... | collective-permute-start | bytes 196616 | tf_op jit(solution)/shard_map/ppermute | solution.py:137
  8.0 23.3 %collective-permute-start = (bf16[768,128]{1,0:T(8,128)(2,1)S(1)}, bf16[768,128]{1,0:T(8,128)(2,1)S(1)}, u32[]{:S(2)}, u32[]{:S(2)}) collective-permute-start(bf16[768,128]{1,0:T(8,128)(2,1)S(1)} %get-tuple-element.37), channel_id=1, source_target_pairs={{0,4},{4,0},{8,12},{12,8},{16,20},{20,16},{24,28},{28,24},{1,5},{5... | collective-permute-start | bytes 589832 | tf_op jit(solution)/shard_map/ppermute | solution.py:137
  8.2 23.8 %collective-permute-start.1 = (bf16[768,128]{1,0:T(8,128)(2,1)S(1)}, bf16[768,128]{1,0:T(8,128)(2,1)S(1)}, u32[]{:S(2)}, u32[]{:S(2)}) collective-permute-start(bf16[768,128]{1,0:T(8,128)(2,1)S(1)} %get-tuple-element.38), channel_id=1, source_target_pairs={{0,8},{4,12},{8,0},{12,4},{16,24},{20,28},{24,16},{28,20},{1,9},{5... | collective-permute-start | bytes 589832 | tf_op jit(solution)/shard_map/ppermute | solution.py:137
  10.1 29.0 %collective-permute-start.2 = (bf16[768,128]{1,0:T(8,128)(2,1)S(1)}, bf16[768,128]{1,0:T(8,128)(2,1)S(1)}, u32[]{:S(2)}, u32[]{:S(2)}) collective-permute-start(bf16[768,128]{1,0:T(8,128)(2,1)S(1)} %get-tuple-element.39), channel_id=1, source_target_pairs={{0,12},{4,8},{8,4},{12,0},{16,28},{20,24},{24,20},{28,16},{1,13},{... | collective-permute-start | bytes 589832 | tf_op jit(solution)/shard_map/ppermute | solution.py:137
  11.5 12.5 %collective-permute-start.5 = (bf16[256,128]{1,0:T(8,128)(2,1)S(1)}, bf16[256,128]{1,0:T(8,128)(2,1)S(1)}, u32[]{:S(2)}, u32[]{:S(2)}) collective-permute-start(bf16[256,128]{1,0:T(8,128)(2,1)S(1)} %get-tuple-element.42), channel_id=1, source_target_pairs={{0,24},{4,28},{8,16},{12,20},{16,8},{20,12},{24,0},{28,4},{1,25},{... | collective-permute-start | bytes 196616 | tf_op jit(solution)/shard_map/ppermute | solution.py:137
  15.6 9.7 %collective-permute-start.6 = (bf16[256,128]{1,0:T(8,128)(2,1)S(1)}, bf16[256,128]{1,0:T(8,128)(2,1)S(1)}, u32[]{:S(2)}, u32[]{:S(2)}) collective-permute-start(bf16[256,128]{1,0:T(8,128)(2,1)S(1)} %get-tuple-element.43), channel_id=1, source_target_pairs={{0,28},{4,24},{8,20},{12,16},{16,12},{20,8},{24,4},{28,0},{1,29},{... | collective-permute-start | bytes 196616 | tf_op jit(solution)/shard_map/ppermute | solution.py:137
  24.0 3.2 %collective-permute-start.10 = (bf16[256,128]{1,0:T(8,128)(2,1)S(1)}, bf16[256,128]{1,0:T(8,128)(2,1)S(1)}, u32[]{:S(2)}, u32[]{:S(2)}) collective-permute-start(bf16[256,128]{1,0:T(8,128)(2,1)S(1)} %get-tuple-element.50), channel_id=1, source_target_pairs={{0,16},{4,20},{8,24},{12,28},{1,17},{5,21},{9,25},{13,29},{2,18},{... | collective-permute-start | bytes 196616 | tf_op jit(solution)/shard_map/ppermute | solution.py:137
  25.3 3.2 %collective-permute-start.11 = (bf16[256,128]{1,0:T(8,128)(2,1)S(1)}, bf16[256,128]{1,0:T(8,128)(2,1)S(1)}, u32[]{:S(2)}, u32[]{:S(2)}) collective-permute-start(bf16[256,128]{1,0:T(8,128)(2,1)S(1)} %get-tuple-element.51), channel_id=1, source_target_pairs={{0,20},{4,16},{8,28},{12,24},{1,21},{5,17},{9,29},{13,25},{2,22},{... | collective-permute-start | bytes 196616 | tf_op jit(solution)/shard_map/ppermute | solution.py:137
  27.1 20.2 %collective-permute-start.7 = (bf16[768,128]{1,0:T(8,128)(2,1)S(1)}, bf16[768,128]{1,0:T(8,128)(2,1)S(1)}, u32[]{:S(2)}, u32[]{:S(2)}) collective-permute-start(bf16[768,128]{1,0:T(8,128)(2,1)S(1)} %get-tuple-element.47), channel_id=1, source_target_pairs={{0,4},{4,0},{8,12},{12,8},{16,20},{20,16},{24,28},{28,24},{1,5},{5... | collective-permute-start | bytes 589832 | tf_op jit(solution)/shard_map/ppermute | solution.py:137
  28.4 18.9 %collective-permute-start.8 = (bf16[768,128]{1,0:T(8,128)(2,1)S(1)}, bf16[768,128]{1,0:T(8,128)(2,1)S(1)}, u32[]{:S(2)}, u32[]{:S(2)}) collective-permute-start(bf16[768,128]{1,0:T(8,128)(2,1)S(1)} %get-tuple-element.48), channel_id=1, source_target_pairs={{0,8},{4,12},{8,0},{12,4},{16,24},{20,28},{24,16},{28,20},{1,9},{5... | collective-permute-start | bytes 589832 | tf_op jit(solution)/shard_map/ppermute | solution.py:137
  31.3 16.1 %collective-permute-start.9 = (bf16[768,128]{1,0:T(8,128)(2,1)S(1)}, bf16[768,128]{1,0:T(8,128)(2,1)S(1)}, u32[]{:S(2)}, u32[]{:S(2)}) collective-permute-start(bf16[768,128]{1,0:T(8,128)(2,1)S(1)} %get-tuple-element.49), channel_id=1, source_target_pairs={{0,12},{4,8},{8,4},{12,0},{16,28},{20,24},{24,20},{28,16},{1,13},{... | collective-permute-start | bytes 589832 | tf_op jit(solution)/shard_map/ppermute | solution.py:137
  32.1 11.2 %collective-permute-start.12 = (bf16[256,128]{1,0:T(8,128)(2,1)S(1)}, bf16[256,128]{1,0:T(8,128)(2,1)S(1)}, u32[]{:S(2)}, u32[]{:S(2)}) collective-permute-start(bf16[256,128]{1,0:T(8,128)(2,1)S(1)} %get-tuple-element.52), channel_id=1, source_target_pairs={{0,24},{4,28},{8,16},{12,20},{1,25},{5,29},{9,17},{13,21},{2,26},{... | collective-permute-start | bytes 196616 | tf_op jit(solution)/shard_map/ppermute | solution.py:137
  39.0 5.6 %collective-permute-start.13 = (bf16[256,128]{1,0:T(8,128)(2,1)S(1)}, bf16[256,128]{1,0:T(8,128)(2,1)S(1)}, u32[]{:S(2)}, u32[]{:S(2)}) collective-permute-start(bf16[256,128]{1,0:T(8,128)(2,1)S(1)} %get-tuple-element.53), channel_id=1, source_target_pairs={{0,28},{4,24},{8,20},{12,16},{1,29},{5,25},{9,21},{13,17},{2,30},{... | collective-permute-start | bytes 196616 | tf_op jit(solution)/shard_map/ppermute | solution.py:137
  43.3 12.3 %collective-permute-start.17 = (bf16[272,128]{1,0:T(8,128)(2,1)S(1)}, bf16[272,128]{1,0:T(8,128)(2,1)S(1)}, u32[]{:S(2)}, u32[]{:S(2)}) collective-permute-start(bf16[272,128]{1,0:T(8,128)(2,1)S(1)} %get-tuple-element.58), channel_id=1, source_target_pairs={{0,16},{4,20},{8,24},{12,28},{1,17},{5,21},{9,25},{13,29},{2,18},{... | collective-permute-start | bytes 208904 | tf_op jit(solution)/shard_map/ppermute | solution.py:137
  44.6 13.4 %collective-permute-start.18 = (bf16[272,128]{1,0:T(8,128)(2,1)S(1)}, bf16[272,128]{1,0:T(8,128)(2,1)S(1)}, u32[]{:S(2)}, u32[]{:S(2)}) collective-permute-start(bf16[272,128]{1,0:T(8,128)(2,1)S(1)} %get-tuple-element.59), channel_id=1, source_target_pairs={{0,20},{4,16},{8,28},{12,24},{1,21},{5,17},{9,29},{13,25},{2,22},{... | collective-permute-start | bytes 208904 | tf_op jit(solution)/shard_map/ppermute | solution.py:137
  51.4 10.2 %collective-permute-start.14 = (bf16[528,128]{1,0:T(8,128)(2,1)S(1)}, bf16[528,128]{1,0:T(8,128)(2,1)S(1)}, u32[]{:S(2)}, u32[]{:S(2)}) collective-permute-start(bf16[528,128]{1,0:T(8,128)(2,1)S(1)} %get-tuple-element.55), channel_id=1, source_target_pairs={{0,4},{4,0},{8,12},{12,8},{16,20},{20,16},{24,28},{28,24},{1,5},{5... | collective-permute-start | bytes 405512 | tf_op jit(solution)/shard_map/ppermute | solution.py:137
  52.6 9.0 %collective-permute-start.15 = (bf16[528,128]{1,0:T(8,128)(2,1)S(1)}, bf16[528,128]{1,0:T(8,128)(2,1)S(1)}, u32[]{:S(2)}, u32[]{:S(2)}) collective-permute-start(bf16[528,128]{1,0:T(8,128)(2,1)S(1)} %get-tuple-element.56), channel_id=1, source_target_pairs={{0,8},{4,12},{8,0},{12,4},{16,24},{20,28},{24,16},{28,20},{1,9},{5... | collective-permute-start | bytes 405512 | tf_op jit(solution)/shard_map/ppermute | solution.py:137
  55.5 6.1 %collective-permute-start.16 = (bf16[528,128]{1,0:T(8,128)(2,1)S(1)}, bf16[528,128]{1,0:T(8,128)(2,1)S(1)}, u32[]{:S(2)}, u32[]{:S(2)}) collective-permute-start(bf16[528,128]{1,0:T(8,128)(2,1)S(1)} %get-tuple-element.57), channel_id=1, source_target_pairs={{0,12},{4,8},{8,4},{12,0},{16,28},{20,24},{24,20},{28,16},{1,13},{... | collective-permute-start | bytes 405512 | tf_op jit(solution)/shard_map/ppermute | solution.py:137
  55.6 5.2 %collective-permute-start.19 = (bf16[272,128]{1,0:T(8,128)(2,1)S(1)}, bf16[272,128]{1,0:T(8,128)(2,1)S(1)}, u32[]{:S(2)}, u32[]{:S(2)}) collective-permute-start(bf16[272,128]{1,0:T(8,128)(2,1)S(1)} %get-tuple-element.60), channel_id=1, source_target_pairs={{0,24},{4,28},{8,16},{12,20},{1,25},{5,29},{9,17},{13,21},{2,26},{... | collective-permute-start | bytes 208904 | tf_op jit(solution)/shard_map/ppermute | solution.py:137
  58.0 3.5 %collective-permute-start.20 = (bf16[272,128]{1,0:T(8,128)(2,1)S(1)}, bf16[272,128]{1,0:T(8,128)(2,1)S(1)}, u32[]{:S(2)}, u32[]{:S(2)}) collective-permute-start(bf16[272,128]{1,0:T(8,128)(2,1)S(1)} %get-tuple-element.61), channel_id=1, source_target_pairs={{0,28},{4,24},{8,20},{12,16},{1,29},{5,25},{9,21},{13,17},{2,30},{... | collective-permute-start | bytes 208904 | tf_op jit(solution)/shard_map/ppermute | solution.py:137
  67.8 4.9 %collective-permute-start.22 = (bf16[256,1024]{1,0:T(8,128)(2,1)S(1)}, bf16[256,1024]{1,0:T(8,128)(2,1)S(1)}, u32[]{:S(2)}, u32[]{:S(2)}) collective-permute-start(bf16[256,1024]{1,0:T(8,128)(2,1)S(1)} %shard_map.70), channel_id=1, source_target_pairs={{0,1},{1,0},{2,3},{3,2},{4,5},{5,4},{6,7},{7,6},{8,9},{9,8},{10,11... | collective-permute-start | bytes 1572872 | tf_op jit(solution)/shard_map/ppermute | solution.py:137
  68.4 9.2 %collective-permute-start.25 = (bf16[256,512]{1,0:T(8,128)(2,1)S(1)}, bf16[256,512]{1,0:T(8,128)(2,1)S(1)}, u32[]{:S(2)}, u32[]{:S(2)}) collective-permute-start(bf16[256,512]{1,0:T(8,128)(2,1)S(1)} %shard_map.69), channel_id=1, source_target_pairs={{0,2},{1,3},{2,0},{3,1},{4,6},{5,7},{6,4},{7,5},{8,10},{9,11},{10,... | collective-permute-start | bytes 786440 | tf_op jit(solution)/shard_map/ppermute | solution.py:137
  71.1 11.2 %collective-permute-start.24 = (bf16[256,512]{1,0:T(8,128)(2,1)S(1)}, bf16[256,512]{1,0:T(8,128)(2,1)S(1)}, u32[]{:S(2)}, u32[]{:S(2)}) collective-permute-start(bf16[256,512]{1,0:T(8,128)(2,1)S(1)} %shard_map.72), channel_id=1, source_target_pairs={{0,2},{1,3},{2,0},{3,1},{4,6},{5,7},{6,4},{7,5},{8,10},{9,11},{10,... | collective-permute-start | bytes 786440 | tf_op jit(solution)/shard_map/ppermute | solution.py:137
  (4 other events, 39.1 us)
where the time goes:
time: 84.7 us; the launch traced here: 83.3 us
  starting transfers between devices  46.8 us (55%)
  waiting for transfers between devices  19.2 us (23%)
  Pallas kernels  16 us (19%)
  other arithmetic  1.03 us (1%)
    ppermute x26, starting transfers between devices, move(): return lax.ppermute(block, axis, pairs)  46.8 us
    ppermute x26, waiting for transfers between devices, move(): return lax.ppermute(block, axis, pairs)  19.2 us
    pallas_call x5, Pallas kernels, columns_of(): own_kernel(functools.partial(project, flip, part, parts), [shape((block,...  5.48 us
    pallas_call x1, Pallas kernels, half_path(): own_kernel(functools.partial(attend_rest, half), [shape((2 * block + STAT...  4.03 us
    pallas_call x1, Pallas kernels, half_path(): own_kernel(functools.partial(attend_low, half), [shape((block + STAT_ROWS...  2.74 us
    pallas_call x1, Pallas kernels, half_path(): own_kernel(functools.partial(deal, half), ([shape((3 * block, HEAD_DIM),...  2.47 us
  transfers between devices with their start and end apart: 26, of which 9 were waited for; matrix products, arithmetic and copies ran while one was open for 0% of the time, Pallas kernels for 11%

commit v1 on v0

--- a/solution.py
+++ b/solution.py
@@ -375,21 +375,28 @@
     me = me_ref[0]
     low = me % half
     block = joined.shape[0]
-    for flip in range(half):
-        at = pl.multiple_of((low ^ flip) * HEAD_DIM, HEAD_DIM)
-        up_at = pl.multiple_of((low ^ flip) * HEAD_DIM + half * HEAD_DIM, HEAD_DIM)
-        joined[:, pl.ds(up_at, HEAD_DIM)] = inner[flip][block : 2 * block]
-
-        @pl.when(me < half)
-        def _():
-            joined[:, pl.ds(at, HEAD_DIM)] = inner[flip][:block]
-
-        @pl.when(me >= half)
-        def _():
+
+    def place(flip, upper, value):
+        at = pl.multiple_of((low ^ flip) * HEAD_DIM + upper * half * HEAD_DIM, HEAD_DIM)
+        joined[:, pl.ds(at, HEAD_DIM)] = value
+
+    @pl.when(me < half)
+    def _():
+        for flip in range(half):
+            place(flip, 0, inner[flip][:block])
+            place(flip, 1, inner[flip][block : 2 * block])
+
+    @pl.when(me >= half)
+    def _():
+        merged = []
+        for flip in range(half):
             share = share_column(inner[flip][2 * block :], across[flip][block:], block)
-            mixed = inner[flip][:block].astype(jnp.float32) * share
-            mixed = mixed + across[flip][:block].astype(jnp.float32) * (1.0 - share)
-            joined[:, pl.ds(at, HEAD_DIM)] = mixed.astype(jnp.bfloat16)
+            value = inner[flip][:block].astype(jnp.float32) * share
+            value = value + across[flip][:block].astype(jnp.float32) * (1.0 - share)
+            merged.append(value.astype(jnp.bfloat16))
+        for flip in range(half):
+            place(flip, 0, merged[flip])
+            place(flip, 1, inner[flip][block : 2 * block])
 
 
 def join_and_project(half, flip, part, parts, me_ref, *refs):
@@ -495,9 +502,9 @@
     first = swap(first, "head", 1)
     second = columns_of(3, 1, parts, joined)
     second = swap(second, "head", 1)
-    far = [first, second]
-    for part in range(parts):
-        far[part] = columns_of(2, part, parts, joined, far[part])
+    kept = columns_of(2, 0, parts, joined)
+    kept = (first.astype(f32) + kept.astype(f32)).astype(bf16)
+    far = [kept, columns_of(2, 1, parts, joined, second)]
     rows, _ = lax.optimization_barrier((joined, far[1]))
     for part in range(parts):
         far[part] = swap(far[part], "head", 2)

time: 84.7 us -> 85.2 us (level)
  waiting for transfers between devices: 19.2 us -> 20.8 us
    ppermute x26, waiting for transfers between devices: 19.2 us -> 20.8 us  [move(): return lax.ppermute(block, axis, pairs)]
  transfers between devices with their start and end apart: 26 -> 26, of which waited for: 9 -> 8; matrix products, arithmetic and copies ran while one was open for 0% -> 0% of each run, Pallas kernels for 11% -> 13%
where the time goes in v1:
time: 85.2 us; the launch traced here: 84.2 us
  starting transfers between devices  46 us (54%)
  waiting for transfers between devices  20.8 us (24%)
  Pallas kernels  16 us (19%)
  other arithmetic  1.1 us (1%)
    ppermute x26, starting transfers between devices, move(): return lax.ppermute(block, axis, pairs)  46 us
    ppermute x26, waiting for transfers between devices, move(): return lax.ppermute(block, axis, pairs)  20.8 us
    pallas_call x5, Pallas kernels, columns_of(): own_kernel(functools.partial(project, flip, part, parts), [shape((block,...  5.48 us
    pallas_call x1, Pallas kernels, half_path(): own_kernel(functools.partial(attend_rest, half), [shape((2 * block + STAT...  4.03 us
    pallas_call x1, Pallas kernels, half_path(): own_kernel(functools.partial(attend_low, half), [shape((block + STAT_ROWS...  2.74 us
    pallas_call x1, Pallas kernels, half_path(): own_kernel(functools.partial(deal, half), ([shape((3 * block, HEAD_DIM),...  2.47 us
  transfers between devices with their start and end apart: 26, of which 8 were waited for; matrix products, arithmetic and copies ran while one was open for 0% of the time, Pallas kernels for 13%

profile of v1, /device:TPU:0, one launch (start us, length us, event | category | flops | bytes accessed | tf_op | source)
XLA Modules:
  0.0 84.2 jit_solution(6058798388221809144)
XLA Ops:
  0.1 2.5 %shard_map.64 = (bf16[768,128]{1,0:T(8,128)(2,1)S(1)}, bf16[768,128]{1,0:T(8,128)(2,1)S(1)}, bf16[768,128]{1,0:T(8,128)(2,1)S(1)}, bf16[768,128]{1,0:T(8,128)(2,...) custom-call(s32[2]{0:T(128)S(1)} %pad_add_fusion.me_ref, ...), custom_call_target="tpu_custom_call" | custom-call | flops 100000000 | bytes 1000000 | tf_op jit(solution)/shard_map/pallas_call | solution.py:434
  2.6 4.1 %collective-permute-start.3 = (bf16[256,128]{1,0:T(8,128)(2,1)S(1)}, bf16[256,128]{1,0:T(8,128)(2,1)S(1)}, u32[]{:S(2)}, u32[]{:S(2)}) collective-permute-start(bf16[256,128]{1,0:T(8,128)(2,1)S(1)} %get-tuple-element.40), channel_id=1, source_target_pairs={{0,16},{4,20},{8,24},{12,28},{16,0},{20,4},{24,8},{28,12},{1,17},{... | collective-permute-start | bytes 196616 | tf_op jit(solution)/shard_map/ppermute | solution.py:137
  8.2 1.8 %collective-permute-start.1 = (bf16[768,128]{1,0:T(8,128)(2,1)S(1)}, bf16[768,128]{1,0:T(8,128)(2,1)S(1)}, u32[]{:S(2)}, u32[]{:S(2)}) collective-permute-start(bf16[768,128]{1,0:T(8,128)(2,1)S(1)} %get-tuple-element.38), channel_id=1, source_target_pairs={{0,8},{4,12},{8,0},{12,4},{16,24},{20,28},{24,16},{28,20},{1,9},{5... | collective-permute-start | bytes 589832 | tf_op jit(solution)/shard_map/ppermute | solution.py:137
  10.1 1.4 %collective-permute-start.2 = (bf16[768,128]{1,0:T(8,128)(2,1)S(1)}, bf16[768,128]{1,0:T(8,128)(2,1)S(1)}, u32[]{:S(2)}, u32[]{:S(2)}) collective-permute-start(bf16[768,128]{1,0:T(8,128)(2,1)S(1)} %get-tuple-element.39), channel_id=1, source_target_pairs={{0,12},{4,8},{8,4},{12,0},{16,28},{20,24},{24,20},{28,16},{1,13},{... | collective-permute-start | bytes 589832 | tf_op jit(solution)/shard_map/ppermute | solution.py:137
  11.5 4.1 %collective-permute-start.5 = (bf16[256,128]{1,0:T(8,128)(2,1)S(1)}, bf16[256,128]{1,0:T(8,128)(2,1)S(1)}, u32[]{:S(2)}, u32[]{:S(2)}) collective-permute-start(bf16[256,128]{1,0:T(8,128)(2,1)S(1)} %get-tuple-element.42), channel_id=1, source_target_pairs={{0,24},{4,28},{8,16},{12,20},{16,8},{20,12},{24,0},{28,4},{1,25},{... | collective-permute-start | bytes 196616 | tf_op jit(solution)/shard_map/ppermute | solution.py:137
  15.6 2.2 %collective-permute-start.6 = (bf16[256,128]{1,0:T(8,128)(2,1)S(1)}, bf16[256,128]{1,0:T(8,128)(2,1)S(1)}, u32[]{:S(2)}, u32[]{:S(2)}) collective-permute-start(bf16[256,128]{1,0:T(8,128)(2,1)S(1)} %get-tuple-element.43), channel_id=1, source_target_pairs={{0,28},{4,24},{8,20},{12,16},{16,12},{20,8},{24,4},{28,0},{1,29},{... | collective-permute-start | bytes 196616 | tf_op jit(solution)/shard_map/ppermute | solution.py:137
  17.8 6.1 %collective-permute-done.5.refs_6_.refs_10_ = bf16[256,128]{1,0:T(8,128)(2,1)S(1)} collective-permute-done((bf16[256,128]{1,0:T(8,128)(2,1)S(1)}, bf16[256,128]{1,0:T(8,128)(2,1)S(1)}, u32[]{:S(2)}, u32[]{:S(2)}) %collective-permute-start.5) | collective-permute-done | bytes 65568 | tf_op jit(solution)/shard_map/ppermute | solution.py:137
  24.0 1.3 %collective-permute-start.10 = (bf16[256,128]{1,0:T(8,128)(2,1)S(1)}, bf16[256,128]{1,0:T(8,128)(2,1)S(1)}, u32[]{:S(2)}, u32[]{:S(2)}) collective-permute-start(bf16[256,128]{1,0:T(8,128)(2,1)S(1)} %get-tuple-element.50), channel_id=1, source_target_pairs={{0,16},{4,20},{8,24},{12,28},{1,17},{5,21},{9,25},{13,29},{2,18},{... | collective-permute-start | bytes 196616 | tf_op jit(solution)/shard_map/ppermute | solution.py:137
  25.3 1.3 %collective-permute-start.11 = (bf16[256,128]{1,0:T(8,128)(2,1)S(1)}, bf16[256,128]{1,0:T(8,128)(2,1)S(1)}, u32[]{:S(2)}, u32[]{:S(2)}) collective-permute-start(bf16[256,128]{1,0:T(8,128)(2,1)S(1)} %get-tuple-element.51), channel_id=1, source_target_pairs={{0,20},{4,16},{8,28},{12,24},{1,21},{5,17},{9,29},{13,25},{2,22},{... | collective-permute-start | bytes 196616 | tf_op jit(solution)/shard_map/ppermute | solution.py:137
  28.4 2.8 %collective-permute-start.8 = (bf16[768,128]{1,0:T(8,128)(2,1)S(1)}, bf16[768,128]{1,0:T(8,128)(2,1)S(1)}, u32[]{:S(2)}, u32[]{:S(2)}) collective-permute-start(bf16[768,128]{1,0:T(8,128)(2,1)S(1)} %get-tuple-element.48), channel_id=1, source_target_pairs={{0,8},{4,12},{8,0},{12,4},{16,24},{20,28},{24,16},{28,20},{1,9},{5... | collective-permute-start | bytes 589832 | tf_op jit(solution)/shard_map/ppermute | solution.py:137
  32.1 6.9 %collective-permute-start.12 = (bf16[256,128]{1,0:T(8,128)(2,1)S(1)}, bf16[256,128]{1,0:T(8,128)(2,1)S(1)}, u32[]{:S(2)}, u32[]{:S(2)}) collective-permute-start(bf16[256,128]{1,0:T(8,128)(2,1)S(1)} %get-tuple-element.52), channel_id=1, source_target_pairs={{0,24},{4,28},{8,16},{12,20},{1,25},{5,29},{9,17},{13,21},{2,26},{... | collective-permute-start | bytes 196616 | tf_op jit(solution)/shard_map/ppermute | solution.py:137
  39.0 1.5 %collective-permute-start.13 = (bf16[256,128]{1,0:T(8,128)(2,1)S(1)}, bf16[256,128]{1,0:T(8,128)(2,1)S(1)}, u32[]{:S(2)}, u32[]{:S(2)}) collective-permute-start(bf16[256,128]{1,0:T(8,128)(2,1)S(1)} %get-tuple-element.53), channel_id=1, source_target_pairs={{0,28},{4,24},{8,20},{12,16},{1,29},{5,25},{9,21},{13,17},{2,30},{... | collective-permute-start | bytes 196616 | tf_op jit(solution)/shard_map/ppermute | solution.py:137
  40.6 2.7 %shard_map.65 = (bf16[272,128]{1,0:T(8,128)(2,1)S(1)}, bf16[272,128]{1,0:T(8,128)(2,1)S(1)}, bf16[272,128]{1,0:T(8,128)(2,1)S(1)}, bf16[272,128]{1,0:T(8,128)(2,...) custom-call(s32[2]{0:T(128)S(1)} %pad_add_fusion.me_ref, ...), custom_call_target="tpu_custom_call" | custom-call | flops 2000000000 | bytes 1000000 | tf_op jit(solution)/shard_map/pallas_call | solution.py:458
  43.3 1.3 %collective-permute-start.17 = (bf16[272,128]{1,0:T(8,128)(2,1)S(1)}, bf16[272,128]{1,0:T(8,128)(2,1)S(1)}, u32[]{:S(2)}, u32[]{:S(2)}) collective-permute-start(bf16[272,128]{1,0:T(8,128)(2,1)S(1)} %get-tuple-element.58), channel_id=1, source_target_pairs={{0,16},{4,20},{8,24},{12,28},{1,17},{5,21},{9,25},{13,29},{2,18},{... | collective-permute-start | bytes 208904 | tf_op jit(solution)/shard_map/ppermute | solution.py:137
  44.6 2.7 %collective-permute-start.18 = (bf16[272,128]{1,0:T(8,128)(2,1)S(1)}, bf16[272,128]{1,0:T(8,128)(2,1)S(1)}, u32[]{:S(2)}, u32[]{:S(2)}) collective-permute-start(bf16[272,128]{1,0:T(8,128)(2,1)S(1)} %get-tuple-element.59), channel_id=1, source_target_pairs={{0,20},{4,16},{8,28},{12,24},{1,21},{5,17},{9,29},{13,25},{2,22},{... | collective-permute-start | bytes 208904 | tf_op jit(solution)/shard_map/ppermute | solution.py:137
  47.3 4.0 %shard_map.66 = (bf16[528,128]{1,0:T(8,128)(2,1)S(1)}, bf16[528,128]{1,0:T(8,128)(2,1)S(1)}, bf16[528,128]{1,0:T(8,128)(2,1)S(1)}, bf16[528,128]{1,0:T(8,128)(2,1)S(1)}) custom-call(s32[2]{0:T(128)S(1)} %pad_add_fusion.me_ref, s32[8,256]{1,0:T(8,128)S(1)} %get-tuple-element.35.reach_ref, bf16[4,256,128]{2,1,0:T(8,128)(2,1)S(1)} %get-tuple-element.44.low_ref, ...), custom_call_target="tpu_custom_call" | custom-call | flops 4000000000 | bytes 1000000 | tf_op jit(solution)/shard_map/pallas_call | solution.py:469
  52.6 2.9 %collective-permute-start.15 = (bf16[528,128]{1,0:T(8,128)(2,1)S(1)}, bf16[528,128]{1,0:T(8,128)(2,1)S(1)}, u32[]{:S(2)}, u32[]{:S(2)}) collective-permute-start(bf16[528,128]{1,0:T(8,128)(2,1)S(1)} %get-tuple-element.56), channel_id=1, source_target_pairs={{0,8},{4,12},{8,0},{12,4},{16,24},{20,28},{24,16},{28,20},{1,9},{5... | collective-permute-start | bytes 405512 | tf_op jit(solution)/shard_map/ppermute | solution.py:137
  55.6 2.4 %collective-permute-start.19 = (bf16[272,128]{1,0:T(8,128)(2,1)S(1)}, bf16[272,128]{1,0:T(8,128)(2,1)S(1)}, u32[]{:S(2)}, u32[]{:S(2)}) collective-permute-start(bf16[272,128]{1,0:T(8,128)(2,1)S(1)} %get-tuple-element.60), channel_id=1, source_target_pairs={{0,24},{4,28},{8,16},{12,20},{1,25},{5,29},{9,17},{13,21},{2,26},{... | collective-permute-start | bytes 208904 | tf_op jit(solution)/shard_map/ppermute | solution.py:137
  58.0 1.4 %collective-permute-start.20 = (bf16[272,128]{1,0:T(8,128)(2,1)S(1)}, bf16[272,128]{1,0:T(8,128)(2,1)S(1)}, u32[]{:S(2)}, u32[]{:S(2)}) collective-permute-start(bf16[272,128]{1,0:T(8,128)(2,1)S(1)} %get-tuple-element.61), channel_id=1, source_target_pairs={{0,28},{4,24},{8,20},{12,16},{1,29},{5,25},{9,21},{13,17},{2,30},{... | collective-permute-start | bytes 208904 | tf_op jit(solution)/shard_map/ppermute | solution.py:137
  59.5 1.3 %collective-permute-done.19.refs_6_ = bf16[272,128]{1,0:T(8,128)(2,1)S(1)} collective-permute-done((bf16[272,128]{1,0:T(8,128)(2,1)S(1)}, bf16[272,128]{1,0:T(8,128)(2,1)S(1)}, u32[]{:S(2)}, u32[]{:S(2)}) %collective-permute-start.19) | collective-permute-done | bytes 69664 | tf_op jit(solution)/shard_map/ppermute | solution.py:137
  61.6 1.3 %shard_map.67 = (bf16[256,512]{1,0:T(8,128)(2,1)S(1)}, bf16[256,1024]{1,0:T(8,128)(2,1)S(1)}) custom-call(s32[2]{0:T(128)S(1)} %pad_add_fusion.me_ref, bf16[528,128]{1,0:T(8,128)(2,1)S(1)} %get-tuple-element.54.refs_0_, bf16[528,128]{1,0:T(8,128)(2,1)S(1)} %collective-permute-done.14.refs_1_, bf16[528,128]{1,0:T(8,128)(2,1)S(1)} %collective-permute-done.15.refs_2_, ...), custom_call_target="tpu_custom_call" | custom-call | flops 1000000000 | bytes 1000000 | tf_op jit(solution)/shard_map/pallas_call | solution.py:496
  69.0 1.6 %collective-permute-start.25 = (bf16[256,512]{1,0:T(8,128)(2,1)S(1)}, bf16[256,512]{1,0:T(8,128)(2,1)S(1)}, u32[]{:S(2)}, u32[]{:S(2)}) collective-permute-start(bf16[256,512]{1,0:T(8,128)(2,1)S(1)} %shard_map.69), channel_id=1, source_target_pairs={{0,2},{1,3},{2,0},{3,1},{4,6},{5,7},{6,4},{7,5},{8,10},{9,11},{10,... | collective-permute-start | bytes 786440 | tf_op jit(solution)/shard_map/ppermute | solution.py:137
  72.5 5.7 %collective-permute-done.25 = bf16[256,512]{1,0:T(8,128)(2,1)S(1)} collective-permute-done((bf16[256,512]{1,0:T(8,128)(2,1)S(1)}, bf16[256,512]{1,0:T(8,128)(2,1)S(1)}, u32[]{:S(2)}, u32[]{:S(2)}) %collective-permute-start.25) | collective-permute-done | bytes 262176 | tf_op jit(solution)/shard_map/ppermute | solution.py:137
  78.2 5.0 %collective-permute-done.24 = bf16[256,512]{1,0:T(8,128)(2,1)S(1)} collective-permute-done((bf16[256,512]{1,0:T(8,128)(2,1)S(1)}, bf16[256,512]{1,0:T(8,128)(2,1)S(1)}, u32[]{:S(2)}, u32[]{:S(2)}) %collective-permute-start.24) | collective-permute-done | bytes 262176 | tf_op jit(solution)/shard_map/ppermute | solution.py:137
  (45 shorter events, 15.4 us)
Async XLA Ops:
  2.6 8.9 %collective-permute-start.3 = (bf16[256,128]{1,0:T(8,128)(2,1)S(1)}, bf16[256,128]{1,0:T(8,128)(2,1)S(1)}, u32[]{:S(2)}, u32[]{:S(2)}) collective-permute-start(bf16[256,128]{1,0:T(8,128)(2,1)S(1)} %get-tuple-element.40), channel_id=1, source_target_pairs={{0,16},{4,20},{8,24},{12,28},{16,0},{20,4},{24,8},{28,12},{1,17},{... | collective-permute-start | bytes 196616 | tf_op jit(solution)/shard_map/ppermute | solution.py:137
  6.7 8.9 %collective-permute-start.4 = (bf16[256,128]{1,0:T(8,128)(2,1)S(1)}, bf16[256,128]{1,0:T(8,128)(2,1)S(1)}, u32[]{:S(2)}, u32[]{:S(2)}) collective-permute-start(bf16[256,128]{1,0:T(8,128)(2,1)S(1)} %get-tuple-element.41), channel_id=1, source_target_pairs={{0,20},{4,16},{8,28},{12,24},{16,4},{20,0},{24,12},{28,8},{1,21},{... | collective-permute-start | bytes 196616 | tf_op jit(solution)/shard_map/ppermute | solution.py:137
  8.0 23.3 %collective-permute-start = (bf16[768,128]{1,0:T(8,128)(2,1)S(1)}, bf16[768,128]{1,0:T(8,128)(2,1)S(1)}, u32[]{:S(2)}, u32[]{:S(2)}) collective-permute-start(bf16[768,128]{1,0:T(8,128)(2,1)S(1)} %get-tuple-element.37), channel_id=1, source_target_pairs={{0,4},{4,0},{8,12},{12,8},{16,20},{20,16},{24,28},{28,24},{1,5},{5... | collective-permute-start | bytes 589832 | tf_op jit(solution)/shard_map/ppermute | solution.py:137
  8.2 23.8 %collective-permute-start.1 = (bf16[768,128]{1,0:T(8,128)(2,1)S(1)}, bf16[768,128]{1,0:T(8,128)(2,1)S(1)}, u32[]{:S(2)}, u32[]{:S(2)}) collective-permute-start(bf16[768,128]{1,0:T(8,128)(2,1)S(1)} %get-tuple-element.38), channel_id=1, source_target_pairs={{0,8},{4,12},{8,0},{12,4},{16,24},{20,28},{24,16},{28,20},{1,9},{5... | collective-permute-start | bytes 589832 | tf_op jit(solution)/shard_map/ppermute | solution.py:137
  10.1 29.0 %collective-permute-start.2 = (bf16[768,128]{1,0:T(8,128)(2,1)S(1)}, bf16[768,128]{1,0:T(8,128)(2,1)S(1)}, u32[]{:S(2)}, u32[]{:S(2)}) collective-permute-start(bf16[768,128]{1,0:T(8,128)(2,1)S(1)} %get-tuple-element.39), channel_id=1, source_target_pairs={{0,12},{4,8},{8,4},{12,0},{16,28},{20,24},{24,20},{28,16},{1,13},{... | collective-permute-start | bytes 589832 | tf_op jit(solution)/shard_map/ppermute | solution.py:137
  11.5 12.5 %collective-permute-start.5 = (bf16[256,128]{1,0:T(8,128)(2,1)S(1)}, bf16[256,128]{1,0:T(8,128)(2,1)S(1)}, u32[]{:S(2)}, u32[]{:S(2)}) collective-permute-start(bf16[256,128]{1,0:T(8,128)(2,1)S(1)} %get-tuple-element.42), channel_id=1, source_target_pairs={{0,24},{4,28},{8,16},{12,20},{16,8},{20,12},{24,0},{28,4},{1,25},{... | collective-permute-start | bytes 196616 | tf_op jit(solution)/shard_map/ppermute | solution.py:137
  15.6 9.7 %collective-permute-start.6 = (bf16[256,128]{1,0:T(8,128)(2,1)S(1)}, bf16[256,128]{1,0:T(8,128)(2,1)S(1)}, u32[]{:S(2)}, u32[]{:S(2)}) collective-permute-start(bf16[256,128]{1,0:T(8,128)(2,1)S(1)} %get-tuple-element.43), channel_id=1, source_target_pairs={{0,28},{4,24},{8,20},{12,16},{16,12},{20,8},{24,4},{28,0},{1,29},{... | collective-permute-start | bytes 196616 | tf_op jit(solution)/shard_map/ppermute | solution.py:137
  25.3 3.2 %collective-permute-start.11 = (bf16[256,128]{1,0:T(8,128)(2,1)S(1)}, bf16[256,128]{1,0:T(8,128)(2,1)S(1)}, u32[]{:S(2)}, u32[]{:S(2)}) collective-permute-start(bf16[256,128]{1,0:T(8,128)(2,1)S(1)} %get-tuple-element.51), channel_id=1, source_target_pairs={{0,20},{4,16},{8,28},{12,24},{1,21},{5,17},{9,29},{13,25},{2,22},{... | collective-permute-start | bytes 196616 | tf_op jit(solution)/shard_map/ppermute | solution.py:137
  27.1 20.2 %collective-permute-start.7 = (bf16[768,128]{1,0:T(8,128)(2,1)S(1)}, bf16[768,128]{1,0:T(8,128)(2,1)S(1)}, u32[]{:S(2)}, u32[]{:S(2)}) collective-permute-start(bf16[768,128]{1,0:T(8,128)(2,1)S(1)} %get-tuple-element.47), channel_id=1, source_target_pairs={{0,4},{4,0},{8,12},{12,8},{16,20},{20,16},{24,28},{28,24},{1,5},{5... | collective-permute-start | bytes 589832 | tf_op jit(solution)/shard_map/ppermute | solution.py:137
  28.4 18.9 %collective-permute-start.8 = (bf16[768,128]{1,0:T(8,128)(2,1)S(1)}, bf16[768,128]{1,0:T(8,128)(2,1)S(1)}, u32[]{:S(2)}, u32[]{:S(2)}) collective-permute-start(bf16[768,128]{1,0:T(8,128)(2,1)S(1)} %get-tuple-element.48), channel_id=1, source_target_pairs={{0,8},{4,12},{8,0},{12,4},{16,24},{20,28},{24,16},{28,20},{1,9},{5... | collective-permute-start | bytes 589832 | tf_op jit(solution)/shard_map/ppermute | solution.py:137
  31.3 16.1 %collective-permute-start.9 = (bf16[768,128]{1,0:T(8,128)(2,1)S(1)}, bf16[768,128]{1,0:T(8,128)(2,1)S(1)}, u32[]{:S(2)}, u32[]{:S(2)}) collective-permute-start(bf16[768,128]{1,0:T(8,128)(2,1)S(1)} %get-tuple-element.49), channel_id=1, source_target_pairs={{0,12},{4,8},{8,4},{12,0},{16,28},{20,24},{24,20},{28,16},{1,13},{... | collective-permute-start | bytes 589832 | tf_op jit(solution)/shard_map/ppermute | solution.py:137
  32.1 11.2 %collective-permute-start.12 = (bf16[256,128]{1,0:T(8,128)(2,1)S(1)}, bf16[256,128]{1,0:T(8,128)(2,1)S(1)}, u32[]{:S(2)}, u32[]{:S(2)}) collective-permute-start(bf16[256,128]{1,0:T(8,128)(2,1)S(1)} %get-tuple-element.52), channel_id=1, source_target_pairs={{0,24},{4,28},{8,16},{12,20},{1,25},{5,29},{9,17},{13,21},{2,26},{... | collective-permute-start | bytes 196616 | tf_op jit(solution)/shard_map/ppermute | solution.py:137
  39.0 5.6 %collective-permute-start.13 = (bf16[256,128]{1,0:T(8,128)(2,1)S(1)}, bf16[256,128]{1,0:T(8,128)(2,1)S(1)}, u32[]{:S(2)}, u32[]{:S(2)}) collective-permute-start(bf16[256,128]{1,0:T(8,128)(2,1)S(1)} %get-tuple-element.53), channel_id=1, source_target_pairs={{0,28},{4,24},{8,20},{12,16},{1,29},{5,25},{9,21},{13,17},{2,30},{... | collective-permute-start | bytes 196616 | tf_op jit(solution)/shard_map/ppermute | solution.py:137
  43.3 12.3 %collective-permute-start.17 = (bf16[272,128]{1,0:T(8,128)(2,1)S(1)}, bf16[272,128]{1,0:T(8,128)(2,1)S(1)}, u32[]{:S(2)}, u32[]{:S(2)}) collective-permute-start(bf16[272,128]{1,0:T(8,128)(2,1)S(1)} %get-tuple-element.58), channel_id=1, source_target_pairs={{0,16},{4,20},{8,24},{12,28},{1,17},{5,21},{9,25},{13,29},{2,18},{... | collective-permute-start | bytes 208904 | tf_op jit(solution)/shard_map/ppermute | solution.py:137
  44.6 13.4 %collective-permute-start.18 = (bf16[272,128]{1,0:T(8,128)(2,1)S(1)}, bf16[272,128]{1,0:T(8,128)(2,1)S(1)}, u32[]{:S(2)}, u32[]{:S(2)}) collective-permute-start(bf16[272,128]{1,0:T(8,128)(2,1)S(1)} %get-tuple-element.59), channel_id=1, source_target_pairs={{0,20},{4,16},{8,28},{12,24},{1,21},{5,17},{9,29},{13,25},{2,22},{... | collective-permute-start | bytes 208904 | tf_op jit(solution)/shard_map/ppermute | solution.py:137
  51.4 10.2 %collective-permute-start.14 = (bf16[528,128]{1,0:T(8,128)(2,1)S(1)}, bf16[528,128]{1,0:T(8,128)(2,1)S(1)}, u32[]{:S(2)}, u32[]{:S(2)}) collective-permute-start(bf16[528,128]{1,0:T(8,128)(2,1)S(1)} %get-tuple-element.55), channel_id=1, source_target_pairs={{0,4},{4,0},{8,12},{12,8},{16,20},{20,16},{24,28},{28,24},{1,5},{5... | collective-permute-start | bytes 405512 | tf_op jit(solution)/shard_map/ppermute | solution.py:137
  52.6 9.0 %collective-permute-start.15 = (bf16[528,128]{1,0:T(8,128)(2,1)S(1)}, bf16[528,128]{1,0:T(8,128)(2,1)S(1)}, u32[]{:S(2)}, u32[]{:S(2)}) collective-permute-start(bf16[528,128]{1,0:T(8,128)(2,1)S(1)} %get-tuple-element.56), channel_id=1, source_target_pairs={{0,8},{4,12},{8,0},{12,4},{16,24},{20,28},{24,16},{28,20},{1,9},{5... | collective-permute-start | bytes 405512 | tf_op jit(solution)/shard_map/ppermute | solution.py:137
  55.5 6.1 %collective-permute-start.16 = (bf16[528,128]{1,0:T(8,128)(2,1)S(1)}, bf16[528,128]{1,0:T(8,128)(2,1)S(1)}, u32[]{:S(2)}, u32[]{:S(2)}) collective-permute-start(bf16[528,128]{1,0:T(8,128)(2,1)S(1)} %get-tuple-element.57), channel_id=1, source_target_pairs={{0,12},{4,8},{8,4},{12,0},{16,28},{20,24},{24,20},{28,16},{1,13},{... | collective-permute-start | bytes 405512 | tf_op jit(solution)/shard_map/ppermute | solution.py:137
  55.6 5.2 %collective-permute-start.19 = (bf16[272,128]{1,0:T(8,128)(2,1)S(1)}, bf16[272,128]{1,0:T(8,128)(2,1)S(1)}, u32[]{:S(2)}, u32[]{:S(2)}) collective-permute-start(bf16[272,128]{1,0:T(8,128)(2,1)S(1)} %get-tuple-element.60), channel_id=1, source_target_pairs={{0,24},{4,28},{8,16},{12,20},{1,25},{5,29},{9,17},{13,21},{2,26},{... | collective-permute-start | bytes 208904 | tf_op jit(solution)/shard_map/ppermute | solution.py:137
  58.0 3.5 %collective-permute-start.20 = (bf16[272,128]{1,0:T(8,128)(2,1)S(1)}, bf16[272,128]{1,0:T(8,128)(2,1)S(1)}, u32[]{:S(2)}, u32[]{:S(2)}) collective-permute-start(bf16[272,128]{1,0:T(8,128)(2,1)S(1)} %get-tuple-element.61), channel_id=1, source_target_pairs={{0,28},{4,24},{8,20},{12,16},{1,29},{5,25},{9,21},{13,17},{2,30},{... | collective-permute-start | bytes 208904 | tf_op jit(solution)/shard_map/ppermute | solution.py:137
  64.0 6.5 %collective-permute-start.23 = (bf16[256,512]{1,0:T(8,128)(2,1)S(1)}, bf16[256,512]{1,0:T(8,128)(2,1)S(1)}, u32[]{:S(2)}, u32[]{:S(2)}) collective-permute-start(bf16[256,512]{1,0:T(8,128)(2,1)S(1)} %get-tuple-element.64), channel_id=1, source_target_pairs={{0,1},{1,0},{2,3},{3,2},{4,5},{5,4},{6,7},{7,6},{8,9},{9,8},{10,11... | collective-permute-start | bytes 786440 | tf_op jit(solution)/shard_map/ppermute | solution.py:137
  67.8 3.4 %collective-permute-start.22 = (bf16[256,1024]{1,0:T(8,128)(2,1)S(1)}, bf16[256,1024]{1,0:T(8,128)(2,1)S(1)}, u32[]{:S(2)}, u32[]{:S(2)}) collective-permute-start(bf16[256,1024]{1,0:T(8,128)(2,1)S(1)} %shard_map.70), channel_id=1, source_target_pairs={{0,1},{1,0},{2,3},{3,2},{4,5},{5,4},{6,7},{7,6},{8,9},{9,8},{10,11... | collective-permute-start | bytes 1572872 | tf_op jit(solution)/shard_map/ppermute | solution.py:137
  69.0 9.2 %collective-permute-start.25 = (bf16[256,512]{1,0:T(8,128)(2,1)S(1)}, bf16[256,512]{1,0:T(8,128)(2,1)S(1)}, u32[]{:S(2)}, u32[]{:S(2)}) collective-permute-start(bf16[256,512]{1,0:T(8,128)(2,1)S(1)} %shard_map.69), channel_id=1, source_target_pairs={{0,2},{1,3},{2,0},{3,1},{4,6},{5,7},{6,4},{7,5},{8,10},{9,11},{10,... | collective-permute-start | bytes 786440 | tf_op jit(solution)/shard_map/ppermute | solution.py:137
  70.6 12.6 %collective-permute-start.24 = (bf16[256,512]{1,0:T(8,128)(2,1)S(1)}, bf16[256,512]{1,0:T(8,128)(2,1)S(1)}, u32[]{:S(2)}, u32[]{:S(2)}) collective-permute-start(bf16[256,512]{1,0:T(8,128)(2,1)S(1)} %add_convert_fusion.1), channel_id=1, source_target_pairs={{0,2},{1,3},{2,0},{3,1},{4,6},{5,7},{6,4},{7,5},{8,10},{9,11},{10,... | collective-permute-start | bytes 786440 | tf_op jit(solution)/shard_map/ppermute | solution.py:137
  (4 other events, 40.1 us)

commit v2 on v1

--- a/solution.py
+++ b/solution.py
@@ -1,6 +1,5 @@
+import functools
 import math
-
-import functools
 
 import jax
 import jax.numpy as jnp
@@ -11,6 +10,7 @@
 
 HEAD_DIM = 128
 SPAN_MAX = 4096
+SPAN_MIN = 1024
 
 
 NEG_FILL = -1e30
@@ -516,8 +516,10 @@
 def on_device(queries, keys_in, values_in, out_weight, spans, full_ids):
     n_seq, n_head = lax.axis_size("seq"), lax.axis_size("head")
     block = queries.shape[0]
-    one_head_each = queries.shape[1] == n_seq * HEAD_DIM
-    if one_head_each and n_head == 4 and n_seq == 8 and block == 256:
+    fits = queries.shape[1] == n_seq * HEAD_DIM and n_seq > 2 and n_seq & (n_seq - 1) == 0
+    fits = fits and block % HEAD_DIM == 0 and n_seq // 2 * block <= SPAN_MIN
+    fits = fits and 3 * block <= STAT_ROWS * HEAD_DIM and n_head == 4
+    if fits:
         return half_path(queries, keys_in, values_in, out_weight, spans, full_ids)
     return ring_path(queries, keys_in, values_in, out_weight, spans, full_ids)
 

time: 85.2 us -> 85.2 us (level)
  no operation moved by 1% of the time
where the time goes in v2:
time: 85.2 us; the launch traced here: 84.2 us
  starting transfers between devices  46 us (54%)
  waiting for transfers between devices  20.8 us (24%)
  Pallas kernels  16 us (19%)
  other arithmetic  1.1 us (1%)
    ppermute x26, starting transfers between devices, move(): return lax.ppermute(block, axis, pairs)  46 us
    ppermute x26, waiting for transfers between devices, move(): return lax.ppermute(block, axis, pairs)  20.8 us
    pallas_call x5, Pallas kernels, columns_of(): own_kernel(functools.partial(project, flip, part, parts), [shape((block,...  5.48 us
    pallas_call x1, Pallas kernels, half_path(): own_kernel(functools.partial(attend_rest, half), [shape((2 * block + STAT...  4.03 us
    pallas_call x1, Pallas kernels, half_path(): own_kernel(functools.partial(attend_low, half), [shape((block + STAT_ROWS...  2.74 us
    pallas_call x1, Pallas kernels, half_path(): own_kernel(functools.partial(deal, half), ([shape((3 * block, HEAD_DIM),...  2.47 us
  transfers between devices with their start and end apart: 26, of which 8 were waited for; matrix products, arithmetic and copies ran while one was open for 0% of the time, Pallas kernels for 13%

profile of v2, /device:TPU:0, one launch (start us, length us, event | category | flops | bytes accessed | tf_op | source)
XLA Modules:
  0.0 84.2 jit_solution(6058798388221809144)
XLA Ops:
  0.1 2.5 %shard_map.64 = (bf16[768,128]{1,0:T(8,128)(2,1)S(1)}, bf16[768,128]{1,0:T(8,128)(2,1)S(1)}, bf16[768,128]{1,0:T(8,128)(2,1)S(1)}, bf16[768,128]{1,0:T(8,128)(2,...) custom-call(s32[2]{0:T(128)S(1)} %pad_add_fusion.me_ref, ...), custom_call_target="tpu_custom_call" | custom-call | flops 100000000 | bytes 1000000 | tf_op jit(solution)/shard_map/pallas_call | solution.py:434
  2.6 4.1 %collective-permute-start.3 = (bf16[256,128]{1,0:T(8,128)(2,1)S(1)}, bf16[256,128]{1,0:T(8,128)(2,1)S(1)}, u32[]{:S(2)}, u32[]{:S(2)}) collective-permute-start(bf16[256,128]{1,0:T(8,128)(2,1)S(1)} %get-tuple-element.40), channel_id=1, source_target_pairs={{0,16},{4,20},{8,24},{12,28},{16,0},{20,4},{24,8},{28,12},{1,17},{... | collective-permute-start | bytes 196616 | tf_op jit(solution)/shard_map/ppermute | solution.py:137
  8.2 1.8 %collective-permute-start.1 = (bf16[768,128]{1,0:T(8,128)(2,1)S(1)}, bf16[768,128]{1,0:T(8,128)(2,1)S(1)}, u32[]{:S(2)}, u32[]{:S(2)}) collective-permute-start(bf16[768,128]{1,0:T(8,128)(2,1)S(1)} %get-tuple-element.38), channel_id=1, source_target_pairs={{0,8},{4,12},{8,0},{12,4},{16,24},{20,28},{24,16},{28,20},{1,9},{5... | collective-permute-start | bytes 589832 | tf_op jit(solution)/shard_map/ppermute | solution.py:137
  10.1 1.4 %collective-permute-start.2 = (bf16[768,128]{1,0:T(8,128)(2,1)S(1)}, bf16[768,128]{1,0:T(8,128)(2,1)S(1)}, u32[]{:S(2)}, u32[]{:S(2)}) collective-permute-start(bf16[768,128]{1,0:T(8,128)(2,1)S(1)} %get-tuple-element.39), channel_id=1, source_target_pairs={{0,12},{4,8},{8,4},{12,0},{16,28},{20,24},{24,20},{28,16},{1,13},{... | collective-permute-start | bytes 589832 | tf_op jit(solution)/shard_map/ppermute | solution.py:137
  11.5 4.1 %collective-permute-start.5 = (bf16[256,128]{1,0:T(8,128)(2,1)S(1)}, bf16[256,128]{1,0:T(8,128)(2,1)S(1)}, u32[]{:S(2)}, u32[]{:S(2)}) collective-permute-start(bf16[256,128]{1,0:T(8,128)(2,1)S(1)} %get-tuple-element.42), channel_id=1, source_target_pairs={{0,24},{4,28},{8,16},{12,20},{16,8},{20,12},{24,0},{28,4},{1,25},{... | collective-permute-start | bytes 196616 | tf_op jit(solution)/shard_map/ppermute | solution.py:137
  15.6 2.2 %collective-permute-start.6 = (bf16[256,128]{1,0:T(8,128)(2,1)S(1)}, bf16[256,128]{1,0:T(8,128)(2,1)S(1)}, u32[]{:S(2)}, u32[]{:S(2)}) collective-permute-start(bf16[256,128]{1,0:T(8,128)(2,1)S(1)} %get-tuple-element.43), channel_id=1, source_target_pairs={{0,28},{4,24},{8,20},{12,16},{16,12},{20,8},{24,4},{28,0},{1,29},{... | collective-permute-start | bytes 196616 | tf_op jit(solution)/shard_map/ppermute | solution.py:137
  17.8 6.1 %collective-permute-done.5.refs_6_.refs_10_ = bf16[256,128]{1,0:T(8,128)(2,1)S(1)} collective-permute-done((bf16[256,128]{1,0:T(8,128)(2,1)S(1)}, bf16[256,128]{1,0:T(8,128)(2,1)S(1)}, u32[]{:S(2)}, u32[]{:S(2)}) %collective-permute-start.5) | collective-permute-done | bytes 65568 | tf_op jit(solution)/shard_map/ppermute | solution.py:137
  24.0 1.3 %collective-permute-start.10 = (bf16[256,128]{1,0:T(8,128)(2,1)S(1)}, bf16[256,128]{1,0:T(8,128)(2,1)S(1)}, u32[]{:S(2)}, u32[]{:S(2)}) collective-permute-start(bf16[256,128]{1,0:T(8,128)(2,1)S(1)} %get-tuple-element.50), channel_id=1, source_target_pairs={{0,16},{4,20},{8,24},{12,28},{1,17},{5,21},{9,25},{13,29},{2,18},{... | collective-permute-start | bytes 196616 | tf_op jit(solution)/shard_map/ppermute | solution.py:137
  25.3 1.3 %collective-permute-start.11 = (bf16[256,128]{1,0:T(8,128)(2,1)S(1)}, bf16[256,128]{1,0:T(8,128)(2,1)S(1)}, u32[]{:S(2)}, u32[]{:S(2)}) collective-permute-start(bf16[256,128]{1,0:T(8,128)(2,1)S(1)} %get-tuple-element.51), channel_id=1, source_target_pairs={{0,20},{4,16},{8,28},{12,24},{1,21},{5,17},{9,29},{13,25},{2,22},{... | collective-permute-start | bytes 196616 | tf_op jit(solution)/shard_map/ppermute | solution.py:137
  28.4 2.8 %collective-permute-start.8 = (bf16[768,128]{1,0:T(8,128)(2,1)S(1)}, bf16[768,128]{1,0:T(8,128)(2,1)S(1)}, u32[]{:S(2)}, u32[]{:S(2)}) collective-permute-start(bf16[768,128]{1,0:T(8,128)(2,1)S(1)} %get-tuple-element.48), channel_id=1, source_target_pairs={{0,8},{4,12},{8,0},{12,4},{16,24},{20,28},{24,16},{28,20},{1,9},{5... | collective-permute-start | bytes 589832 | tf_op jit(solution)/shard_map/ppermute | solution.py:137
  32.1 6.9 %collective-permute-start.12 = (bf16[256,128]{1,0:T(8,128)(2,1)S(1)}, bf16[256,128]{1,0:T(8,128)(2,1)S(1)}, u32[]{:S(2)}, u32[]{:S(2)}) collective-permute-start(bf16[256,128]{1,0:T(8,128)(2,1)S(1)} %get-tuple-element.52), channel_id=1, source_target_pairs={{0,24},{4,28},{8,16},{12,20},{1,25},{5,29},{9,17},{13,21},{2,26},{... | collective-permute-start | bytes 196616 | tf_op jit(solution)/shard_map/ppermute | solution.py:137
  39.0 1.5 %collective-permute-start.13 = (bf16[256,128]{1,0:T(8,128)(2,1)S(1)}, bf16[256,128]{1,0:T(8,128)(2,1)S(1)}, u32[]{:S(2)}, u32[]{:S(2)}) collective-permute-start(bf16[256,128]{1,0:T(8,128)(2,1)S(1)} %get-tuple-element.53), channel_id=1, source_target_pairs={{0,28},{4,24},{8,20},{12,16},{1,29},{5,25},{9,21},{13,17},{2,30},{... | collective-permute-start | bytes 196616 | tf_op jit(solution)/shard_map/ppermute | solution.py:137
  40.6 2.7 %shard_map.65 = (bf16[272,128]{1,0:T(8,128)(2,1)S(1)}, bf16[272,128]{1,0:T(8,128)(2,1)S(1)}, bf16[272,128]{1,0:T(8,128)(2,1)S(1)}, bf16[272,128]{1,0:T(8,128)(2,...) custom-call(s32[2]{0:T(128)S(1)} %pad_add_fusion.me_ref, ...), custom_call_target="tpu_custom_call" | custom-call | flops 2000000000 | bytes 1000000 | tf_op jit(solution)/shard_map/pallas_call | solution.py:458
  43.3 1.3 %collective-permute-start.17 = (bf16[272,128]{1,0:T(8,128)(2,1)S(1)}, bf16[272,128]{1,0:T(8,128)(2,1)S(1)}, u32[]{:S(2)}, u32[]{:S(2)}) collective-permute-start(bf16[272,128]{1,0:T(8,128)(2,1)S(1)} %get-tuple-element.58), channel_id=1, source_target_pairs={{0,16},{4,20},{8,24},{12,28},{1,17},{5,21},{9,25},{13,29},{2,18},{... | collective-permute-start | bytes 208904 | tf_op jit(solution)/shard_map/ppermute | solution.py:137
  44.6 2.7 %collective-permute-start.18 = (bf16[272,128]{1,0:T(8,128)(2,1)S(1)}, bf16[272,128]{1,0:T(8,128)(2,1)S(1)}, u32[]{:S(2)}, u32[]{:S(2)}) collective-permute-start(bf16[272,128]{1,0:T(8,128)(2,1)S(1)} %get-tuple-element.59), channel_id=1, source_target_pairs={{0,20},{4,16},{8,28},{12,24},{1,21},{5,17},{9,29},{13,25},{2,22},{... | collective-permute-start | bytes 208904 | tf_op jit(solution)/shard_map/ppermute | solution.py:137
  47.3 4.0 %shard_map.66 = (bf16[528,128]{1,0:T(8,128)(2,1)S(1)}, bf16[528,128]{1,0:T(8,128)(2,1)S(1)}, bf16[528,128]{1,0:T(8,128)(2,1)S(1)}, bf16[528,128]{1,0:T(8,128)(2,1)S(1)}) custom-call(s32[2]{0:T(128)S(1)} %pad_add_fusion.me_ref, s32[8,256]{1,0:T(8,128)S(1)} %get-tuple-element.35.reach_ref, bf16[4,256,128]{2,1,0:T(8,128)(2,1)S(1)} %get-tuple-element.44.low_ref, ...), custom_call_target="tpu_custom_call" | custom-call | flops 4000000000 | bytes 1000000 | tf_op jit(solution)/shard_map/pallas_call | solution.py:469
  52.6 2.9 %collective-permute-start.15 = (bf16[528,128]{1,0:T(8,128)(2,1)S(1)}, bf16[528,128]{1,0:T(8,128)(2,1)S(1)}, u32[]{:S(2)}, u32[]{:S(2)}) collective-permute-start(bf16[528,128]{1,0:T(8,128)(2,1)S(1)} %get-tuple-element.56), channel_id=1, source_target_pairs={{0,8},{4,12},{8,0},{12,4},{16,24},{20,28},{24,16},{28,20},{1,9},{5... | collective-permute-start | bytes 405512 | tf_op jit(solution)/shard_map/ppermute | solution.py:137
  55.6 2.4 %collective-permute-start.19 = (bf16[272,128]{1,0:T(8,128)(2,1)S(1)}, bf16[272,128]{1,0:T(8,128)(2,1)S(1)}, u32[]{:S(2)}, u32[]{:S(2)}) collective-permute-start(bf16[272,128]{1,0:T(8,128)(2,1)S(1)} %get-tuple-element.60), channel_id=1, source_target_pairs={{0,24},{4,28},{8,16},{12,20},{1,25},{5,29},{9,17},{13,21},{2,26},{... | collective-permute-start | bytes 208904 | tf_op jit(solution)/shard_map/ppermute | solution.py:137
  58.0 1.4 %collective-permute-start.20 = (bf16[272,128]{1,0:T(8,128)(2,1)S(1)}, bf16[272,128]{1,0:T(8,128)(2,1)S(1)}, u32[]{:S(2)}, u32[]{:S(2)}) collective-permute-start(bf16[272,128]{1,0:T(8,128)(2,1)S(1)} %get-tuple-element.61), channel_id=1, source_target_pairs={{0,28},{4,24},{8,20},{12,16},{1,29},{5,25},{9,21},{13,17},{2,30},{... | collective-permute-start | bytes 208904 | tf_op jit(solution)/shard_map/ppermute | solution.py:137
  59.5 1.3 %collective-permute-done.19.refs_6_ = bf16[272,128]{1,0:T(8,128)(2,1)S(1)} collective-permute-done((bf16[272,128]{1,0:T(8,128)(2,1)S(1)}, bf16[272,128]{1,0:T(8,128)(2,1)S(1)}, u32[]{:S(2)}, u32[]{:S(2)}) %collective-permute-start.19) | collective-permute-done | bytes 69664 | tf_op jit(solution)/shard_map/ppermute | solution.py:137
  61.6 1.3 %shard_map.67 = (bf16[256,512]{1,0:T(8,128)(2,1)S(1)}, bf16[256,1024]{1,0:T(8,128)(2,1)S(1)}) custom-call(s32[2]{0:T(128)S(1)} %pad_add_fusion.me_ref, bf16[528,128]{1,0:T(8,128)(2,1)S(1)} %get-tuple-element.54.refs_0_, bf16[528,128]{1,0:T(8,128)(2,1)S(1)} %collective-permute-done.14.refs_1_, bf16[528,128]{1,0:T(8,128)(2,1)S(1)} %collective-permute-done.15.refs_2_, ...), custom_call_target="tpu_custom_call" | custom-call | flops 1000000000 | bytes 1000000 | tf_op jit(solution)/shard_map/pallas_call | solution.py:496
  69.0 1.6 %collective-permute-start.25 = (bf16[256,512]{1,0:T(8,128)(2,1)S(1)}, bf16[256,512]{1,0:T(8,128)(2,1)S(1)}, u32[]{:S(2)}, u32[]{:S(2)}) collective-permute-start(bf16[256,512]{1,0:T(8,128)(2,1)S(1)} %shard_map.69), channel_id=1, source_target_pairs={{0,2},{1,3},{2,0},{3,1},{4,6},{5,7},{6,4},{7,5},{8,10},{9,11},{10,... | collective-permute-start | bytes 786440 | tf_op jit(solution)/shard_map/ppermute | solution.py:137
  72.5 5.7 %collective-permute-done.25 = bf16[256,512]{1,0:T(8,128)(2,1)S(1)} collective-permute-done((bf16[256,512]{1,0:T(8,128)(2,1)S(1)}, bf16[256,512]{1,0:T(8,128)(2,1)S(1)}, u32[]{:S(2)}, u32[]{:S(2)}) %collective-permute-start.25) | collective-permute-done | bytes 262176 | tf_op jit(solution)/shard_map/ppermute | solution.py:137
  78.2 5.0 %collective-permute-done.24 = bf16[256,512]{1,0:T(8,128)(2,1)S(1)} collective-permute-done((bf16[256,512]{1,0:T(8,128)(2,1)S(1)}, bf16[256,512]{1,0:T(8,128)(2,1)S(1)}, u32[]{:S(2)}, u32[]{:S(2)}) %collective-permute-start.24) | collective-permute-done | bytes 262176 | tf_op jit(solution)/shard_map/ppermute | solution.py:137
  (45 shorter events, 15.4 us)
Async XLA Ops:
  2.6 8.9 %collective-permute-start.3 = (bf16[256,128]{1,0:T(8,128)(2,1)S(1)}, bf16[256,128]{1,0:T(8,128)(2,1)S(1)}, u32[]{:S(2)}, u32[]{:S(2)}) collective-permute-start(bf16[256,128]{1,0:T(8,128)(2,1)S(1)} %get-tuple-element.40), channel_id=1, source_target_pairs={{0,16},{4,20},{8,24},{12,28},{16,0},{20,4},{24,8},{28,12},{1,17},{... | collective-permute-start | bytes 196616 | tf_op jit(solution)/shard_map/ppermute | solution.py:137
  6.7 8.9 %collective-permute-start.4 = (bf16[256,128]{1,0:T(8,128)(2,1)S(1)}, bf16[256,128]{1,0:T(8,128)(2,1)S(1)}, u32[]{:S(2)}, u32[]{:S(2)}) collective-permute-start(bf16[256,128]{1,0:T(8,128)(2,1)S(1)} %get-tuple-element.41), channel_id=1, source_target_pairs={{0,20},{4,16},{8,28},{12,24},{16,4},{20,0},{24,12},{28,8},{1,21},{... | collective-permute-start | bytes 196616 | tf_op jit(solution)/shard_map/ppermute | solution.py:137
  8.0 23.3 %collective-permute-start = (bf16[768,128]{1,0:T(8,128)(2,1)S(1)}, bf16[768,128]{1,0:T(8,128)(2,1)S(1)}, u32[]{:S(2)}, u32[]{:S(2)}) collective-permute-start(bf16[768,128]{1,0:T(8,128)(2,1)S(1)} %get-tuple-element.37), channel_id=1, source_target_pairs={{0,4},{4,0},{8,12},{12,8},{16,20},{20,16},{24,28},{28,24},{1,5},{5... | collective-permute-start | bytes 589832 | tf_op jit(solution)/shard_map/ppermute | solution.py:137
  8.2 23.8 %collective-permute-start.1 = (bf16[768,128]{1,0:T(8,128)(2,1)S(1)}, bf16[768,128]{1,0:T(8,128)(2,1)S(1)}, u32[]{:S(2)}, u32[]{:S(2)}) collective-permute-start(bf16[768,128]{1,0:T(8,128)(2,1)S(1)} %get-tuple-element.38), channel_id=1, source_target_pairs={{0,8},{4,12},{8,0},{12,4},{16,24},{20,28},{24,16},{28,20},{1,9},{5... | collective-permute-start | bytes 589832 | tf_op jit(solution)/shard_map/ppermute | solution.py:137
  10.1 29.0 %collective-permute-start.2 = (bf16[768,128]{1,0:T(8,128)(2,1)S(1)}, bf16[768,128]{1,0:T(8,128)(2,1)S(1)}, u32[]{:S(2)}, u32[]{:S(2)}) collective-permute-start(bf16[768,128]{1,0:T(8,128)(2,1)S(1)} %get-tuple-element.39), channel_id=1, source_target_pairs={{0,12},{4,8},{8,4},{12,0},{16,28},{20,24},{24,20},{28,16},{1,13},{... | collective-permute-start | bytes 589832 | tf_op jit(solution)/shard_map/ppermute | solution.py:137
  11.5 12.5 %collective-permute-start.5 = (bf16[256,128]{1,0:T(8,128)(2,1)S(1)}, bf16[256,128]{1,0:T(8,128)(2,1)S(1)}, u32[]{:S(2)}, u32[]{:S(2)}) collective-permute-start(bf16[256,128]{1,0:T(8,128)(2,1)S(1)} %get-tuple-element.42), channel_id=1, source_target_pairs={{0,24},{4,28},{8,16},{12,20},{16,8},{20,12},{24,0},{28,4},{1,25},{... | collective-permute-start | bytes 196616 | tf_op jit(solution)/shard_map/ppermute | solution.py:137
  15.6 9.7 %collective-permute-start.6 = (bf16[256,128]{1,0:T(8,128)(2,1)S(1)}, bf16[256,128]{1,0:T(8,128)(2,1)S(1)}, u32[]{:S(2)}, u32[]{:S(2)}) collective-permute-start(bf16[256,128]{1,0:T(8,128)(2,1)S(1)} %get-tuple-element.43), channel_id=1, source_target_pairs={{0,28},{4,24},{8,20},{12,16},{16,12},{20,8},{24,4},{28,0},{1,29},{... | collective-permute-start | bytes 196616 | tf_op jit(solution)/shard_map/ppermute | solution.py:137
  25.3 3.2 %collective-permute-start.11 = (bf16[256,128]{1,0:T(8,128)(2,1)S(1)}, bf16[256,128]{1,0:T(8,128)(2,1)S(1)}, u32[]{:S(2)}, u32[]{:S(2)}) collective-permute-start(bf16[256,128]{1,0:T(8,128)(2,1)S(1)} %get-tuple-element.51), channel_id=1, source_target_pairs={{0,20},{4,16},{8,28},{12,24},{1,21},{5,17},{9,29},{13,25},{2,22},{... | collective-permute-start | bytes 196616 | tf_op jit(solution)/shard_map/ppermute | solution.py:137
  27.1 20.2 %collective-permute-start.7 = (bf16[768,128]{1,0:T(8,128)(2,1)S(1)}, bf16[768,128]{1,0:T(8,128)(2,1)S(1)}, u32[]{:S(2)}, u32[]{:S(2)}) collective-permute-start(bf16[768,128]{1,0:T(8,128)(2,1)S(1)} %get-tuple-element.47), channel_id=1, source_target_pairs={{0,4},{4,0},{8,12},{12,8},{16,20},{20,16},{24,28},{28,24},{1,5},{5... | collective-permute-start | bytes 589832 | tf_op jit(solution)/shard_map/ppermute | solution.py:137
  28.4 18.9 %collective-permute-start.8 = (bf16[768,128]{1,0:T(8,128)(2,1)S(1)}, bf16[768,128]{1,0:T(8,128)(2,1)S(1)}, u32[]{:S(2)}, u32[]{:S(2)}) collective-permute-start(bf16[768,128]{1,0:T(8,128)(2,1)S(1)} %get-tuple-element.48), channel_id=1, source_target_pairs={{0,8},{4,12},{8,0},{12,4},{16,24},{20,28},{24,16},{28,20},{1,9},{5... | collective-permute-start | bytes 589832 | tf_op jit(solution)/shard_map/ppermute | solution.py:137
  31.3 16.1 %collective-permute-start.9 = (bf16[768,128]{1,0:T(8,128)(2,1)S(1)}, bf16[768,128]{1,0:T(8,128)(2,1)S(1)}, u32[]{:S(2)}, u32[]{:S(2)}) collective-permute-start(bf16[768,128]{1,0:T(8,128)(2,1)S(1)} %get-tuple-element.49), channel_id=1, source_target_pairs={{0,12},{4,8},{8,4},{12,0},{16,28},{20,24},{24,20},{28,16},{1,13},{... | collective-permute-start | bytes 589832 | tf_op jit(solution)/shard_map/ppermute | solution.py:137
  32.1 11.2 %collective-permute-start.12 = (bf16[256,128]{1,0:T(8,128)(2,1)S(1)}, bf16[256,128]{1,0:T(8,128)(2,1)S(1)}, u32[]{:S(2)}, u32[]{:S(2)}) collective-permute-start(bf16[256,128]{1,0:T(8,128)(2,1)S(1)} %get-tuple-element.52), channel_id=1, source_target_pairs={{0,24},{4,28},{8,16},{12,20},{1,25},{5,29},{9,17},{13,21},{2,26},{... | collective-permute-start | bytes 196616 | tf_op jit(solution)/shard_map/ppermute | solution.py:137
  39.0 5.6 %collective-permute-start.13 = (bf16[256,128]{1,0:T(8,128)(2,1)S(1)}, bf16[256,128]{1,0:T(8,128)(2,1)S(1)}, u32[]{:S(2)}, u32[]{:S(2)}) collective-permute-start(bf16[256,128]{1,0:T(8,128)(2,1)S(1)} %get-tuple-element.53), channel_id=1, source_target_pairs={{0,28},{4,24},{8,20},{12,16},{1,29},{5,25},{9,21},{13,17},{2,30},{... | collective-permute-start | bytes 196616 | tf_op jit(solution)/shard_map/ppermute | solution.py:137
  43.3 12.3 %collective-permute-start.17 = (bf16[272,128]{1,0:T(8,128)(2,1)S(1)}, bf16[272,128]{1,0:T(8,128)(2,1)S(1)}, u32[]{:S(2)}, u32[]{:S(2)}) collective-permute-start(bf16[272,128]{1,0:T(8,128)(2,1)S(1)} %get-tuple-element.58), channel_id=1, source_target_pairs={{0,16},{4,20},{8,24},{12,28},{1,17},{5,21},{9,25},{13,29},{2,18},{... | collective-permute-start | bytes 208904 | tf_op jit(solution)/shard_map/ppermute | solution.py:137
  44.6 13.4 %collective-permute-start.18 = (bf16[272,128]{1,0:T(8,128)(2,1)S(1)}, bf16[272,128]{1,0:T(8,128)(2,1)S(1)}, u32[]{:S(2)}, u32[]{:S(2)}) collective-permute-start(bf16[272,128]{1,0:T(8,128)(2,1)S(1)} %get-tuple-element.59), channel_id=1, source_target_pairs={{0,20},{4,16},{8,28},{12,24},{1,21},{5,17},{9,29},{13,25},{2,22},{... | collective-permute-start | bytes 208904 | tf_op jit(solution)/shard_map/ppermute | solution.py:137
  51.4 10.2 %collective-permute-start.14 = (bf16[528,128]{1,0:T(8,128)(2,1)S(1)}, bf16[528,128]{1,0:T(8,128)(2,1)S(1)}, u32[]{:S(2)}, u32[]{:S(2)}) collective-permute-start(bf16[528,128]{1,0:T(8,128)(2,1)S(1)} %get-tuple-element.55), channel_id=1, source_target_pairs={{0,4},{4,0},{8,12},{12,8},{16,20},{20,16},{24,28},{28,24},{1,5},{5... | collective-permute-start | bytes 405512 | tf_op jit(solution)/shard_map/ppermute | solution.py:137
  52.6 9.0 %collective-permute-start.15 = (bf16[528,128]{1,0:T(8,128)(2,1)S(1)}, bf16[528,128]{1,0:T(8,128)(2,1)S(1)}, u32[]{:S(2)}, u32[]{:S(2)}) collective-permute-start(bf16[528,128]{1,0:T(8,128)(2,1)S(1)} %get-tuple-element.56), channel_id=1, source_target_pairs={{0,8},{4,12},{8,0},{12,4},{16,24},{20,28},{24,16},{28,20},{1,9},{5... | collective-permute-start | bytes 405512 | tf_op jit(solution)/shard_map/ppermute | solution.py:137
  55.5 6.1 %collective-permute-start.16 = (bf16[528,128]{1,0:T(8,128)(2,1)S(1)}, bf16[528,128]{1,0:T(8,128)(2,1)S(1)}, u32[]{:S(2)}, u32[]{:S(2)}) collective-permute-start(bf16[528,128]{1,0:T(8,128)(2,1)S(1)} %get-tuple-element.57), channel_id=1, source_target_pairs={{0,12},{4,8},{8,4},{12,0},{16,28},{20,24},{24,20},{28,16},{1,13},{... | collective-permute-start | bytes 405512 | tf_op jit(solution)/shard_map/ppermute | solution.py:137
  55.6 5.2 %collective-permute-start.19 = (bf16[272,128]{1,0:T(8,128)(2,1)S(1)}, bf16[272,128]{1,0:T(8,128)(2,1)S(1)}, u32[]{:S(2)}, u32[]{:S(2)}) collective-permute-start(bf16[272,128]{1,0:T(8,128)(2,1)S(1)} %get-tuple-element.60), channel_id=1, source_target_pairs={{0,24},{4,28},{8,16},{12,20},{1,25},{5,29},{9,17},{13,21},{2,26},{... | collective-permute-start | bytes 208904 | tf_op jit(solution)/shard_map/ppermute | solution.py:137
  58.0 3.5 %collective-permute-start.20 = (bf16[272,128]{1,0:T(8,128)(2,1)S(1)}, bf16[272,128]{1,0:T(8,128)(2,1)S(1)}, u32[]{:S(2)}, u32[]{:S(2)}) collective-permute-start(bf16[272,128]{1,0:T(8,128)(2,1)S(1)} %get-tuple-element.61), channel_id=1, source_target_pairs={{0,28},{4,24},{8,20},{12,16},{1,29},{5,25},{9,21},{13,17},{2,30},{... | collective-permute-start | bytes 208904 | tf_op jit(solution)/shard_map/ppermute | solution.py:137
  64.0 6.5 %collective-permute-start.23 = (bf16[256,512]{1,0:T(8,128)(2,1)S(1)}, bf16[256,512]{1,0:T(8,128)(2,1)S(1)}, u32[]{:S(2)}, u32[]{:S(2)}) collective-permute-start(bf16[256,512]{1,0:T(8,128)(2,1)S(1)} %get-tuple-element.64), channel_id=1, source_target_pairs={{0,1},{1,0},{2,3},{3,2},{4,5},{5,4},{6,7},{7,6},{8,9},{9,8},{10,11... | collective-permute-start | bytes 786440 | tf_op jit(solution)/shard_map/ppermute | solution.py:137
  67.8 3.4 %collective-permute-start.22 = (bf16[256,1024]{1,0:T(8,128)(2,1)S(1)}, bf16[256,1024]{1,0:T(8,128)(2,1)S(1)}, u32[]{:S(2)}, u32[]{:S(2)}) collective-permute-start(bf16[256,1024]{1,0:T(8,128)(2,1)S(1)} %shard_map.70), channel_id=1, source_target_pairs={{0,1},{1,0},{2,3},{3,2},{4,5},{5,4},{6,7},{7,6},{8,9},{9,8},{10,11... | collective-permute-start | bytes 1572872 | tf_op jit(solution)/shard_map/ppermute | solution.py:137
  69.0 9.2 %collective-permute-start.25 = (bf16[256,512]{1,0:T(8,128)(2,1)S(1)}, bf16[256,512]{1,0:T(8,128)(2,1)S(1)}, u32[]{:S(2)}, u32[]{:S(2)}) collective-permute-start(bf16[256,512]{1,0:T(8,128)(2,1)S(1)} %shard_map.69), channel_id=1, source_target_pairs={{0,2},{1,3},{2,0},{3,1},{4,6},{5,7},{6,4},{7,5},{8,10},{9,11},{10,... | collective-permute-start | bytes 786440 | tf_op jit(solution)/shard_map/ppermute | solution.py:137
  70.6 12.6 %collective-permute-start.24 = (bf16[256,512]{1,0:T(8,128)(2,1)S(1)}, bf16[256,512]{1,0:T(8,128)(2,1)S(1)}, u32[]{:S(2)}, u32[]{:S(2)}) collective-permute-start(bf16[256,512]{1,0:T(8,128)(2,1)S(1)} %add_convert_fusion.1), channel_id=1, source_target_pairs={{0,2},{1,3},{2,0},{3,1},{4,6},{5,7},{6,4},{7,5},{8,10},{9,11},{10,... | collective-permute-start | bytes 786440 | tf_op jit(solution)/shard_map/ppermute | solution.py:137
  (4 other events, 40.1 us)
